TPU v7x, 16 devices: a whole 2x2x2 slice. The times are simulated.
16 devices in a mesh: rep: 4 (over z, y), shard: 4 (over x, core).
Axes of the slice: x: 2, y: 2, z: 2, core: 2. Of those that a mesh axis runs over, the one named last changes fastest.
Arguments:
- ratings: float32 [10240, 512], P(('rep', 'shard')), parts along dimension 0
- obs_mask: int32 [10240, 512], P(('rep', 'shard')), parts along dimension 0
- step_counts: int32 [16, 4], P(('rep', 'shard')), parts along dimension 0
- user_init: float32 [10240, 256], P(('rep', 'shard')), parts along dimension 0
- item_init: float32 [2048, 256], P(('rep', 'shard')), parts along dimension 0
Outputs:
- output 1: float32 [10240, 256], P(('rep', 'shard')), parts along dimension 0
- output 2: float32 [2048, 256], P(('rep', 'shard')), parts along dimension 0
There are 4 independent parts. A program takes and returns all parts, laid end to end along the dimension named above; each array names one.
All inputs are finite; a program needn't handle non-finite values.
Results may differ from a plain program's by a relative error of at most 0.00155027.
Values are sent between devices in bfloat16 or wider.
A program may use at most 1 GiB of HBM per device.

v0:
```python
import math
import jax
import jax.numpy as jnp
from jax import lax
from jax.sharding import PartitionSpec as P

EPOCHS = 2


def solution(mesh):
    group_size = mesh.shape["shard"]
    row_spec = P(("rep", "shard"), None)
    shift_perm = [(source, (source - 1) % group_size) for source in range(group_size)]

    def local_run(ratings, obs_mask, step_counts, user_init, item_init):
        users_dev, rank_dim = user_init.shape
        items_dev = item_init.shape[0]
        step_size = 0.4 * math.sqrt(rank_dim) / (users_dev + rank_dim)
        decay_rate = 0.1 * items_dev / math.sqrt(rank_dim)
        dev_index = lax.axis_index("shard")
        step_row = step_counts[0]

        def sub_epoch(sweep_idx, carry_in):
            user_cur, item_cur = carry_in
            col_id = (dev_index + sweep_idx) % group_size
            rating_blk = lax.dynamic_slice_in_dim(ratings, col_id * items_dev, items_dev, axis=1)
            seen_blk = lax.dynamic_slice_in_dim(obs_mask, col_id * items_dev, items_dev, axis=1) != 0

            def grad_step(step_idx, inner_in):
                user_now, item_now = inner_in
                user_half = user_now.astype(jnp.bfloat16)
                item_half = item_now.astype(jnp.bfloat16)
                approx = jnp.einsum("ur,ir->ui", user_half, item_half, preferred_element_type=jnp.float32)
                err_half = jnp.where(seen_blk, approx - rating_blk, 0.0).astype(jnp.bfloat16)
                grad_user = jnp.einsum("ui,ir->ur", err_half, item_half, preferred_element_type=jnp.float32) + decay_rate * user_now
                grad_item = jnp.einsum("ui,ur->ir", err_half, user_half, preferred_element_type=jnp.float32) + decay_rate * item_now
                return user_now - step_size * grad_user, item_now - step_size * grad_item

            user_new, item_new = lax.fori_loop(0, step_row[col_id], grad_step, (user_cur, item_cur))
            return user_new, lax.ppermute(item_new, "shard", shift_perm)

        return lax.fori_loop(0, EPOCHS * group_size, sub_epoch, (user_init, item_init))

    return jax.shard_map(local_run, mesh=mesh, in_specs=(row_spec,) * 5, out_specs=(row_spec, row_spec), check_vma=False)
```

profile of v0, /device:TPU:7, one launch (start us, length us, event | category | flops | bytes accessed | tf_op | source)
XLA Modules:
  0.0 93.2 jit_solution(566737627124635672)
XLA Ops:
  0.7 0.6 copy-done.4
  1.3 0.4 copy-done.1
  1.7 90.6 %while.53 = (s32[]{:T(128)}, f32[640,256]{1,0:T(8,128)S(1)}, f32[128,256]{1,0:T(8,128)S(1)}, s32[]{:T(128)}, s32[4]{0:T(128)S(1)}, /*index=5*/f32[640,512]{1,0:T...) while((s32[]{:T(128)}, f32[640,256]{1,0:T(8,128)S(1)}, ...), condition=%wide.region_3.4_spmd, body=%wide.region_0.3_spmd.sunk | while | flops 127336464 | bytes 6160919 | solution.py:42
  1.7 1.0 %dynamic-slice_compare_fusion.2 = pred[640,128]{1,0:T(32,128)(4,1)S(1)} fusion(s32[640,512]{1,0:T(8,128)} %get-tuple-element.400, s32[]{:T(128)S(6)} %select_n.54), kind=kLoop, calls=%fused_computation.13.clone.1 | loop fusion | flops 81920 | bytes 409604 | tf_op jit(solution)/shard_map/while/body/eval_jaxpr/ne | solution.py:27
  2.8 1.0 %constant_dynamic-slice_fusion.2 = f32[640,128]{1,0:T(8,128)S(1)} fusion(f32[640,512]{1,0:T(8,128)} %get-tuple-element.399, s32[]{:T(128)S(6)} %select_n.54), kind=kLoop, calls=%fused_computation.14.clone.1 | loop fusion | bytes 655364 | tf_op jit(solution)/shard_map/while/body/eval_jaxpr/dynamic_slice | solution.py:26
  3.8 0.6 dynamic_slice.37
  4.4 2.0 %while.54 = (s32[]{:T(128)}, f32[640,256]{1,0:T(8,128)S(1)}, f32[128,256]{1,0:T(8,128)S(1)}, s32[]{:T(128)}, f32[640,128]{1,0:T(8,128)S(1)}, /*index=5*/pred[640,128]{1,0:T(32,128)(4,1)S(1)}, s32[]{:T(128)}) while((s32[]{:T(128)}, f32[640,256]{1,0:T(8,128)S(1)}, f32[128,256]{1,0:T(8,128)S(1)}, s32[]{:T(128)}, f32[640,128]{1,0:T(8,128)S(1)}, ...), condition=%wide.region_2.2_spmd, body=%wide.region_1.1_spmd.sunk | while | flops 127254528 | bytes 4309069 | solution.py:39
  5.5 0.3 fusion.28
  6.4 5.0 %collective-permute-start = (f32[128,256]{1,0:T(8,128)S(1)}, f32[128,256]{1,0:T(8,128)S(1)}, u32[]{:S(2)}, u32[]{:S(2)}) collective-permute-start(f32[128,256]{1,0:T(8,128)S(1)} %get-tuple-element.337), channel_id=1, source_target_pairs={{0,3},{1,0},{2,1},{3,2},{4,7},{5,4},{6,5},{7,6},{8,11},{9,8},{10,9... | collective-permute-start | bytes 393224 | tf_op jit(solution)/shard_map/while/body/eval_jaxpr/ppermute | solution.py:40
  11.4 1.0 %collective-permute-done = f32[128,256]{1,0:T(8,128)S(1)} collective-permute-done((f32[128,256]{1,0:T(8,128)S(1)}, f32[128,256]{1,0:T(8,128)S(1)}, u32[]{:S(2)}, u32[]{:S(2)}) %collective-permute-start) | collective-permute-done | bytes 131104 | tf_op jit(solution)/shard_map/while/body/eval_jaxpr/ppermute | solution.py:40
  12.4 1.0 %dynamic-slice_compare_fusion.2 = pred[640,128]{1,0:T(32,128)(4,1)S(1)} fusion(s32[640,512]{1,0:T(8,128)} %get-tuple-element.400, s32[]{:T(128)S(6)} %select_n.54), kind=kLoop, calls=%fused_computation.13.clone.1 | loop fusion | flops 81920 | bytes 409604 | tf_op jit(solution)/shard_map/while/body/eval_jaxpr/ne | solution.py:27
  13.4 1.0 %constant_dynamic-slice_fusion.2 = f32[640,128]{1,0:T(8,128)S(1)} fusion(f32[640,512]{1,0:T(8,128)} %get-tuple-element.399, s32[]{:T(128)S(6)} %select_n.54), kind=kLoop, calls=%fused_computation.14.clone.1 | loop fusion | bytes 655364 | tf_op jit(solution)/shard_map/while/body/eval_jaxpr/dynamic_slice | solution.py:26
  14.4 0.6 dynamic_slice.37
  15.0 3.4 %while.54 = (s32[]{:T(128)}, f32[640,256]{1,0:T(8,128)S(1)}, f32[128,256]{1,0:T(8,128)S(1)}, s32[]{:T(128)}, f32[640,128]{1,0:T(8,128)S(1)}, /*index=5*/pred[640,128]{1,0:T(32,128)(4,1)S(1)}, s32[]{:T(128)}) while((s32[]{:T(128)}, f32[640,256]{1,0:T(8,128)S(1)}, f32[128,256]{1,0:T(8,128)S(1)}, s32[]{:T(128)}, f32[640,128]{1,0:T(8,128)S(1)}, ...), condition=%wide.region_2.2_spmd, body=%wide.region_1.1_spmd.sunk | while | flops 127254528 | bytes 4309069 | solution.py:39
  16.1 0.3 fusion.28
  17.5 0.3 fusion.28
  18.4 4.4 %collective-permute-start = (f32[128,256]{1,0:T(8,128)S(1)}, f32[128,256]{1,0:T(8,128)S(1)}, u32[]{:S(2)}, u32[]{:S(2)}) collective-permute-start(f32[128,256]{1,0:T(8,128)S(1)} %get-tuple-element.337), channel_id=1, source_target_pairs={{0,3},{1,0},{2,1},{3,2},{4,7},{5,4},{6,5},{7,6},{8,11},{9,8},{10,9... | collective-permute-start | bytes 393224 | tf_op jit(solution)/shard_map/while/body/eval_jaxpr/ppermute | solution.py:40
  22.9 1.0 %collective-permute-done = f32[128,256]{1,0:T(8,128)S(1)} collective-permute-done((f32[128,256]{1,0:T(8,128)S(1)}, f32[128,256]{1,0:T(8,128)S(1)}, u32[]{:S(2)}, u32[]{:S(2)}) %collective-permute-start) | collective-permute-done | bytes 131104 | tf_op jit(solution)/shard_map/while/body/eval_jaxpr/ppermute | solution.py:40
  23.9 1.0 %dynamic-slice_compare_fusion.2 = pred[640,128]{1,0:T(32,128)(4,1)S(1)} fusion(s32[640,512]{1,0:T(8,128)} %get-tuple-element.400, s32[]{:T(128)S(6)} %select_n.54), kind=kLoop, calls=%fused_computation.13.clone.1 | loop fusion | flops 81920 | bytes 409604 | tf_op jit(solution)/shard_map/while/body/eval_jaxpr/ne | solution.py:27
  25.0 1.0 %constant_dynamic-slice_fusion.2 = f32[640,128]{1,0:T(8,128)S(1)} fusion(f32[640,512]{1,0:T(8,128)} %get-tuple-element.399, s32[]{:T(128)S(6)} %select_n.54), kind=kLoop, calls=%fused_computation.14.clone.1 | loop fusion | bytes 655364 | tf_op jit(solution)/shard_map/while/body/eval_jaxpr/dynamic_slice | solution.py:26
  26.0 0.6 dynamic_slice.37
  26.5 6.3 %while.54 = (s32[]{:T(128)}, f32[640,256]{1,0:T(8,128)S(1)}, f32[128,256]{1,0:T(8,128)S(1)}, s32[]{:T(128)}, f32[640,128]{1,0:T(8,128)S(1)}, /*index=5*/pred[640,128]{1,0:T(32,128)(4,1)S(1)}, s32[]{:T(128)}) while((s32[]{:T(128)}, f32[640,256]{1,0:T(8,128)S(1)}, f32[128,256]{1,0:T(8,128)S(1)}, s32[]{:T(128)}, f32[640,128]{1,0:T(8,128)S(1)}, ...), condition=%wide.region_2.2_spmd, body=%wide.region_1.1_spmd.sunk | while | flops 127254528 | bytes 4309069 | solution.py:39
  29.1 0.3 fusion.28
  30.5 0.3 fusion.28
  31.9 0.3 fusion.28
  32.9 4.4 %collective-permute-done = f32[128,256]{1,0:T(8,128)S(1)} collective-permute-done((f32[128,256]{1,0:T(8,128)S(1)}, f32[128,256]{1,0:T(8,128)S(1)}, u32[]{:S(2)}, u32[]{:S(2)}) %collective-permute-start) | collective-permute-done | bytes 131104 | tf_op jit(solution)/shard_map/while/body/eval_jaxpr/ppermute | solution.py:40
  37.3 1.0 %dynamic-slice_compare_fusion.2 = pred[640,128]{1,0:T(32,128)(4,1)S(1)} fusion(s32[640,512]{1,0:T(8,128)} %get-tuple-element.400, s32[]{:T(128)S(6)} %select_n.54), kind=kLoop, calls=%fused_computation.13.clone.1 | loop fusion | flops 81920 | bytes 409604 | tf_op jit(solution)/shard_map/while/body/eval_jaxpr/ne | solution.py:27
  38.3 1.0 %constant_dynamic-slice_fusion.2 = f32[640,128]{1,0:T(8,128)S(1)} fusion(f32[640,512]{1,0:T(8,128)} %get-tuple-element.399, s32[]{:T(128)S(6)} %select_n.54), kind=kLoop, calls=%fused_computation.14.clone.1 | loop fusion | bytes 655364 | tf_op jit(solution)/shard_map/while/body/eval_jaxpr/dynamic_slice | solution.py:26
  39.4 0.6 dynamic_slice.37
  39.9 3.4 %while.54 = (s32[]{:T(128)}, f32[640,256]{1,0:T(8,128)S(1)}, f32[128,256]{1,0:T(8,128)S(1)}, s32[]{:T(128)}, f32[640,128]{1,0:T(8,128)S(1)}, /*index=5*/pred[640,128]{1,0:T(32,128)(4,1)S(1)}, s32[]{:T(128)}) while((s32[]{:T(128)}, f32[640,256]{1,0:T(8,128)S(1)}, f32[128,256]{1,0:T(8,128)S(1)}, s32[]{:T(128)}, f32[640,128]{1,0:T(8,128)S(1)}, ...), condition=%wide.region_2.2_spmd, body=%wide.region_1.1_spmd.sunk | while | flops 127254528 | bytes 4309069 | solution.py:39
  41.0 0.3 fusion.28
  43.4 4.4 %collective-permute-done = f32[128,256]{1,0:T(8,128)S(1)} collective-permute-done((f32[128,256]{1,0:T(8,128)S(1)}, f32[128,256]{1,0:T(8,128)S(1)}, u32[]{:S(2)}, u32[]{:S(2)}) %collective-permute-start) | collective-permute-done | bytes 131104 | tf_op jit(solution)/shard_map/while/body/eval_jaxpr/ppermute | solution.py:40
  47.9 1.0 %dynamic-slice_compare_fusion.2 = pred[640,128]{1,0:T(32,128)(4,1)S(1)} fusion(s32[640,512]{1,0:T(8,128)} %get-tuple-element.400, s32[]{:T(128)S(6)} %select_n.54), kind=kLoop, calls=%fused_computation.13.clone.1 | loop fusion | flops 81920 | bytes 409604 | tf_op jit(solution)/shard_map/while/body/eval_jaxpr/ne | solution.py:27
  48.9 1.0 %constant_dynamic-slice_fusion.2 = f32[640,128]{1,0:T(8,128)S(1)} fusion(f32[640,512]{1,0:T(8,128)} %get-tuple-element.399, s32[]{:T(128)S(6)} %select_n.54), kind=kLoop, calls=%fused_computation.14.clone.1 | loop fusion | bytes 655364 | tf_op jit(solution)/shard_map/while/body/eval_jaxpr/dynamic_slice | solution.py:26
  49.9 0.6 dynamic_slice.37
  50.5 2.0 %while.54 = (s32[]{:T(128)}, f32[640,256]{1,0:T(8,128)S(1)}, f32[128,256]{1,0:T(8,128)S(1)}, s32[]{:T(128)}, f32[640,128]{1,0:T(8,128)S(1)}, /*index=5*/pred[640,128]{1,0:T(32,128)(4,1)S(1)}, s32[]{:T(128)}) while((s32[]{:T(128)}, f32[640,256]{1,0:T(8,128)S(1)}, f32[128,256]{1,0:T(8,128)S(1)}, s32[]{:T(128)}, f32[640,128]{1,0:T(8,128)S(1)}, ...), condition=%wide.region_2.2_spmd, body=%wide.region_1.1_spmd.sunk | while | flops 127254528 | bytes 4309069 | solution.py:39
  51.6 0.3 fusion.28
  52.5 1.6 %collective-permute-start = (f32[128,256]{1,0:T(8,128)S(1)}, f32[128,256]{1,0:T(8,128)S(1)}, u32[]{:S(2)}, u32[]{:S(2)}) collective-permute-start(f32[128,256]{1,0:T(8,128)S(1)} %get-tuple-element.337), channel_id=1, source_target_pairs={{0,3},{1,0},{2,1},{3,2},{4,7},{5,4},{6,5},{7,6},{8,11},{9,8},{10,9... | collective-permute-start | bytes 393224 | tf_op jit(solution)/shard_map/while/body/eval_jaxpr/ppermute | solution.py:40
  54.1 2.9 %collective-permute-done = f32[128,256]{1,0:T(8,128)S(1)} collective-permute-done((f32[128,256]{1,0:T(8,128)S(1)}, f32[128,256]{1,0:T(8,128)S(1)}, u32[]{:S(2)}, u32[]{:S(2)}) %collective-permute-start) | collective-permute-done | bytes 131104 | tf_op jit(solution)/shard_map/while/body/eval_jaxpr/ppermute | solution.py:40
  57.0 1.0 %dynamic-slice_compare_fusion.2 = pred[640,128]{1,0:T(32,128)(4,1)S(1)} fusion(s32[640,512]{1,0:T(8,128)} %get-tuple-element.400, s32[]{:T(128)S(6)} %select_n.54), kind=kLoop, calls=%fused_computation.13.clone.1 | loop fusion | flops 81920 | bytes 409604 | tf_op jit(solution)/shard_map/while/body/eval_jaxpr/ne | solution.py:27
  58.0 1.0 %constant_dynamic-slice_fusion.2 = f32[640,128]{1,0:T(8,128)S(1)} fusion(f32[640,512]{1,0:T(8,128)} %get-tuple-element.399, s32[]{:T(128)S(6)} %select_n.54), kind=kLoop, calls=%fused_computation.14.clone.1 | loop fusion | bytes 655364 | tf_op jit(solution)/shard_map/while/body/eval_jaxpr/dynamic_slice | solution.py:26
  59.0 0.6 dynamic_slice.37
  59.6 3.4 %while.54 = (s32[]{:T(128)}, f32[640,256]{1,0:T(8,128)S(1)}, f32[128,256]{1,0:T(8,128)S(1)}, s32[]{:T(128)}, f32[640,128]{1,0:T(8,128)S(1)}, /*index=5*/pred[640,128]{1,0:T(32,128)(4,1)S(1)}, s32[]{:T(128)}) while((s32[]{:T(128)}, f32[640,256]{1,0:T(8,128)S(1)}, f32[128,256]{1,0:T(8,128)S(1)}, s32[]{:T(128)}, f32[640,128]{1,0:T(8,128)S(1)}, ...), condition=%wide.region_2.2_spmd, body=%wide.region_1.1_spmd.sunk | while | flops 127254528 | bytes 4309069 | solution.py:39
  60.7 0.3 fusion.28
  62.1 0.3 fusion.28
  63.0 4.4 %collective-permute-start = (f32[128,256]{1,0:T(8,128)S(1)}, f32[128,256]{1,0:T(8,128)S(1)}, u32[]{:S(2)}, u32[]{:S(2)}) collective-permute-start(f32[128,256]{1,0:T(8,128)S(1)} %get-tuple-element.337), channel_id=1, source_target_pairs={{0,3},{1,0},{2,1},{3,2},{4,7},{5,4},{6,5},{7,6},{8,11},{9,8},{10,9... | collective-permute-start | bytes 393224 | tf_op jit(solution)/shard_map/while/body/eval_jaxpr/ppermute | solution.py:40
  67.4 1.0 %collective-permute-done = f32[128,256]{1,0:T(8,128)S(1)} collective-permute-done((f32[128,256]{1,0:T(8,128)S(1)}, f32[128,256]{1,0:T(8,128)S(1)}, u32[]{:S(2)}, u32[]{:S(2)}) %collective-permute-start) | collective-permute-done | bytes 131104 | tf_op jit(solution)/shard_map/while/body/eval_jaxpr/ppermute | solution.py:40
  68.5 1.0 %dynamic-slice_compare_fusion.2 = pred[640,128]{1,0:T(32,128)(4,1)S(1)} fusion(s32[640,512]{1,0:T(8,128)} %get-tuple-element.400, s32[]{:T(128)S(6)} %select_n.54), kind=kLoop, calls=%fused_computation.13.clone.1 | loop fusion | flops 81920 | bytes 409604 | tf_op jit(solution)/shard_map/while/body/eval_jaxpr/ne | solution.py:27
  69.5 1.0 %constant_dynamic-slice_fusion.2 = f32[640,128]{1,0:T(8,128)S(1)} fusion(f32[640,512]{1,0:T(8,128)} %get-tuple-element.399, s32[]{:T(128)S(6)} %select_n.54), kind=kLoop, calls=%fused_computation.14.clone.1 | loop fusion | bytes 655364 | tf_op jit(solution)/shard_map/while/body/eval_jaxpr/dynamic_slice | solution.py:26
  70.5 0.6 dynamic_slice.37
  71.1 6.3 %while.54 = (s32[]{:T(128)}, f32[640,256]{1,0:T(8,128)S(1)}, f32[128,256]{1,0:T(8,128)S(1)}, s32[]{:T(128)}, f32[640,128]{1,0:T(8,128)S(1)}, /*index=5*/pred[640,128]{1,0:T(32,128)(4,1)S(1)}, s32[]{:T(128)}) while((s32[]{:T(128)}, f32[640,256]{1,0:T(8,128)S(1)}, f32[128,256]{1,0:T(8,128)S(1)}, s32[]{:T(128)}, f32[640,128]{1,0:T(8,128)S(1)}, ...), condition=%wide.region_2.2_spmd, body=%wide.region_1.1_spmd.sunk | while | flops 127254528 | bytes 4309069 | solution.py:39
  72.2 0.3 fusion.28
  73.6 0.3 fusion.28
  75.1 0.3 fusion.28
  76.5 0.3 fusion.28
  77.4 4.4 %collective-permute-done = f32[128,256]{1,0:T(8,128)S(1)} collective-permute-done((f32[128,256]{1,0:T(8,128)S(1)}, f32[128,256]{1,0:T(8,128)S(1)}, u32[]{:S(2)}, u32[]{:S(2)}) %collective-permute-start) | collective-permute-done | bytes 131104 | tf_op jit(solution)/shard_map/while/body/eval_jaxpr/ppermute | solution.py:40
  81.9 1.0 %dynamic-slice_compare_fusion.2 = pred[640,128]{1,0:T(32,128)(4,1)S(1)} fusion(s32[640,512]{1,0:T(8,128)} %get-tuple-element.400, s32[]{:T(128)S(6)} %select_n.54), kind=kLoop, calls=%fused_computation.13.clone.1 | loop fusion | flops 81920 | bytes 409604 | tf_op jit(solution)/shard_map/while/body/eval_jaxpr/ne | solution.py:27
  82.9 1.0 %constant_dynamic-slice_fusion.2 = f32[640,128]{1,0:T(8,128)S(1)} fusion(f32[640,512]{1,0:T(8,128)} %get-tuple-element.399, s32[]{:T(128)S(6)} %select_n.54), kind=kLoop, calls=%fused_computation.14.clone.1 | loop fusion | bytes 655364 | tf_op jit(solution)/shard_map/while/body/eval_jaxpr/dynamic_slice | solution.py:26
  83.9 0.6 dynamic_slice.37
  84.5 3.4 %while.54 = (s32[]{:T(128)}, f32[640,256]{1,0:T(8,128)S(1)}, f32[128,256]{1,0:T(8,128)S(1)}, s32[]{:T(128)}, f32[640,128]{1,0:T(8,128)S(1)}, /*index=5*/pred[640,128]{1,0:T(32,128)(4,1)S(1)}, s32[]{:T(128)}) while((s32[]{:T(128)}, f32[640,256]{1,0:T(8,128)S(1)}, f32[128,256]{1,0:T(8,128)S(1)}, s32[]{:T(128)}, f32[640,128]{1,0:T(8,128)S(1)}, ...), condition=%wide.region_2.2_spmd, body=%wide.region_1.1_spmd.sunk | while | flops 127254528 | bytes 4309069 | solution.py:39
  85.6 0.3 fusion.28
  87.0 0.3 fusion.28
  88.0 4.4 %collective-permute-done = f32[128,256]{1,0:T(8,128)S(1)} collective-permute-done((f32[128,256]{1,0:T(8,128)S(1)}, f32[128,256]{1,0:T(8,128)S(1)}, u32[]{:S(2)}, u32[]{:S(2)}) %collective-permute-start) | collective-permute-done | bytes 131104 | tf_op jit(solution)/shard_map/while/body/eval_jaxpr/ppermute | solution.py:40
  92.4 0.8 copy-done
  (75 shorter events, 10.3 us)
Async XLA Ops:
  0.6 0.7 copy-start.4
  0.6 1.1 %copy-start.1 = (f32[640,256]{1,0:T(8,128)S(1)}, f32[640,256]{1,0:T(8,128)}, u32[]{:S(2)}) copy-start(f32[640,256]{1,0:T(8,128)} %param.12) | copy-start | bytes 1966084
  0.7 1.1 %copy-start.3 = (f32[128,256]{1,0:T(8,128)S(1)}, f32[128,256]{1,0:T(8,128)}, u32[]{:S(2)}) copy-start(f32[128,256]{1,0:T(8,128)} %param.13) | copy-start | bytes 393220
  6.4 6.0 %collective-permute-start = (f32[128,256]{1,0:T(8,128)S(1)}, f32[128,256]{1,0:T(8,128)S(1)}, u32[]{:S(2)}, u32[]{:S(2)}) collective-permute-start(f32[128,256]{1,0:T(8,128)S(1)} %get-tuple-element.337), channel_id=1, source_target_pairs={{0,3},{1,0},{2,1},{3,2},{4,7},{5,4},{6,5},{7,6},{8,11},{9,8},{10,9... | collective-permute-start | bytes 393224 | tf_op jit(solution)/shard_map/while/body/eval_jaxpr/ppermute | solution.py:40
  18.4 5.4 %collective-permute-start = (f32[128,256]{1,0:T(8,128)S(1)}, f32[128,256]{1,0:T(8,128)S(1)}, u32[]{:S(2)}, u32[]{:S(2)}) collective-permute-start(f32[128,256]{1,0:T(8,128)S(1)} %get-tuple-element.337), channel_id=1, source_target_pairs={{0,3},{1,0},{2,1},{3,2},{4,7},{5,4},{6,5},{7,6},{8,11},{9,8},{10,9... | collective-permute-start | bytes 393224 | tf_op jit(solution)/shard_map/while/body/eval_jaxpr/ppermute | solution.py:40
  32.8 4.4 %collective-permute-start = (f32[128,256]{1,0:T(8,128)S(1)}, f32[128,256]{1,0:T(8,128)S(1)}, u32[]{:S(2)}, u32[]{:S(2)}) collective-permute-start(f32[128,256]{1,0:T(8,128)S(1)} %get-tuple-element.337), channel_id=1, source_target_pairs={{0,3},{1,0},{2,1},{3,2},{4,7},{5,4},{6,5},{7,6},{8,11},{9,8},{10,9... | collective-permute-start | bytes 393224 | tf_op jit(solution)/shard_map/while/body/eval_jaxpr/ppermute | solution.py:40
  43.4 4.4 %collective-permute-start = (f32[128,256]{1,0:T(8,128)S(1)}, f32[128,256]{1,0:T(8,128)S(1)}, u32[]{:S(2)}, u32[]{:S(2)}) collective-permute-start(f32[128,256]{1,0:T(8,128)S(1)} %get-tuple-element.337), channel_id=1, source_target_pairs={{0,3},{1,0},{2,1},{3,2},{4,7},{5,4},{6,5},{7,6},{8,11},{9,8},{10,9... | collective-permute-start | bytes 393224 | tf_op jit(solution)/shard_map/while/body/eval_jaxpr/ppermute | solution.py:40
  52.5 4.4 %collective-permute-start = (f32[128,256]{1,0:T(8,128)S(1)}, f32[128,256]{1,0:T(8,128)S(1)}, u32[]{:S(2)}, u32[]{:S(2)}) collective-permute-start(f32[128,256]{1,0:T(8,128)S(1)} %get-tuple-element.337), channel_id=1, source_target_pairs={{0,3},{1,0},{2,1},{3,2},{4,7},{5,4},{6,5},{7,6},{8,11},{9,8},{10,9... | collective-permute-start | bytes 393224 | tf_op jit(solution)/shard_map/while/body/eval_jaxpr/ppermute | solution.py:40
  63.0 5.4 %collective-permute-start = (f32[128,256]{1,0:T(8,128)S(1)}, f32[128,256]{1,0:T(8,128)S(1)}, u32[]{:S(2)}, u32[]{:S(2)}) collective-permute-start(f32[128,256]{1,0:T(8,128)S(1)} %get-tuple-element.337), channel_id=1, source_target_pairs={{0,3},{1,0},{2,1},{3,2},{4,7},{5,4},{6,5},{7,6},{8,11},{9,8},{10,9... | collective-permute-start | bytes 393224 | tf_op jit(solution)/shard_map/while/body/eval_jaxpr/ppermute | solution.py:40
  77.4 4.4 %collective-permute-start = (f32[128,256]{1,0:T(8,128)S(1)}, f32[128,256]{1,0:T(8,128)S(1)}, u32[]{:S(2)}, u32[]{:S(2)}) collective-permute-start(f32[128,256]{1,0:T(8,128)S(1)} %get-tuple-element.337), channel_id=1, source_target_pairs={{0,3},{1,0},{2,1},{3,2},{4,7},{5,4},{6,5},{7,6},{8,11},{9,8},{10,9... | collective-permute-start | bytes 393224 | tf_op jit(solution)/shard_map/while/body/eval_jaxpr/ppermute | solution.py:40
  87.9 4.4 %collective-permute-start = (f32[128,256]{1,0:T(8,128)S(1)}, f32[128,256]{1,0:T(8,128)S(1)}, u32[]{:S(2)}, u32[]{:S(2)}) collective-permute-start(f32[128,256]{1,0:T(8,128)S(1)} %get-tuple-element.337), channel_id=1, source_target_pairs={{0,3},{1,0},{2,1},{3,2},{4,7},{5,4},{6,5},{7,6},{8,11},{9,8},{10,9... | collective-permute-start | bytes 393224 | tf_op jit(solution)/shard_map/while/body/eval_jaxpr/ppermute | solution.py:40
  92.4 0.8 copy-start
  92.4 0.9 copy-start.2
where the time goes:
time: 105 us; the launch traced here: 93.2 us
  waiting for transfers between devices  35 us (33%)
  matrix products  22.9 us (22%)
  loops' own time  21.8 us (21%)
  local copies, waits for them, and re-layouts  15 us (14%)
  other arithmetic  8.19 us (8%)
    ppermute x8, waiting for transfers between devices, sub_epoch(): return (user_new, lax.ppermute(item_new, 'shard', shift_perm))  35 us
    another operation x8, loops' own time, sub_epoch(): lax.fori_loop(0, step_row[col_id], grad_step, (user_cur, item_cur))  21.2 us
    dot_general x28, matrix products, grad_step(): jnp.einsum('ui,ir->ur', err_half, item_half, preferred_element_type=jnp.f...  8.69 us
    ne x8, other arithmetic, sub_epoch(): lax.dynamic_slice_in_dim(obs_mask, col_id * items_dev, items_dev, axis=1)  8.19 us
    dynamic_slice x8, local copies, waits for them, and re-layouts, sub_epoch(): lax.dynamic_slice_in_dim(ratings, col_id * items_dev, items_dev, axis=1)  8.01 us
    dot_general x28, matrix products, grad_step(): jnp.einsum('ui,ur->ir', err_half, user_half, preferred_element_type=jnp.f...  7.16 us
    dot_general x28, matrix products, grad_step(): jnp.einsum('ur,ir->ui', user_half, item_half, preferred_element_type=jnp....  7.06 us
    dynamic_slice x8, local copies, waits for them, and re-layouts, sub_epoch(): step_row[col_id]  4.64 us
  transfers between devices with their start and end apart: 8, of which 8 were waited for; matrix products, arithmetic and copies ran while one was open for 0% of the time, Pallas kernels for 0%

commit v1 on v0

v1 whole, which is shorter than its diff:
```python
import math
import jax
import jax.numpy as jnp
from jax import lax
from jax.experimental import pallas as pl
from jax.experimental.pallas import tpu as pltpu
from jax.sharding import PartitionSpec as P

EPOCHS = 2
STEPS_MAX = 4
CHUNK = 128


def make_kernel(n, users, items, rank):
    step_size = 0.4 * math.sqrt(rank) / (users + rank)
    decay = 0.1 * items / math.sqrt(rank)
    keep = 1.0 - step_size * decay
    hops = EPOCHS * n
    bf16, f32 = jnp.bfloat16, jnp.float32
    starts = range(0, users, CHUNK)

    def kernel(cnt, r_hbm, m_hbm, u_hbm, v_hbm, u_out, v_out,
               r_buf, m_buf, u_f, u_b, v_slot, v_send, v_f, e_b,
               r_sem, m_sem, u_sem, recv_sem, send_sem, out_sem):
        me = lax.axis_index("shard")
        left, right = lax.rem(me + n - 1, n), lax.rem(me + 1, n)

        barrier = pltpu.get_barrier_semaphore()
        for peer in (left, right):
            pl.semaphore_signal(barrier, inc=1, device_id={"shard": peer}, device_id_type=pl.DeviceIdType.MESH)

        def block_copy(kind, q):
            src, dst, sem = ((r_hbm, r_buf, r_sem), (m_hbm, m_buf, m_sem))[kind]
            col = pl.multiple_of(lax.rem(me + q, n) * items, items)
            return pltpu.make_async_copy(src.at[:, pl.ds(col, items)], dst.at[q], sem.at[q])

        u_in = pltpu.make_async_copy(u_hbm, u_f, u_sem)
        v_in = pltpu.make_async_copy(v_hbm, v_slot.at[0], recv_sem.at[0])
        u_in.start()
        v_in.start()
        for q in range(n):
            block_copy(0, q).start()
            block_copy(1, q).start()
        u_in.wait()
        for s in starts:
            u_b[pl.ds(s, CHUNK), :] = u_f[pl.ds(s, CHUNK), :].astype(bf16)
        v_in.wait()
        pl.semaphore_wait(barrier, 2)

        def hop_copy(t):
            return pltpu.make_async_remote_copy(
                src_ref=v_send.at[t], dst_ref=v_slot.at[t + 1],
                send_sem=send_sem.at[t], recv_sem=recv_sem.at[t + 1],
                device_id={"shard": left}, device_id_type=pl.DeviceIdType.MESH)

        def sub_epoch(t, carry):
            q = lax.rem(t, n)
            count = cnt[0, lax.rem(me + t, n)]

            @pl.when(t < n)
            def _():
                block_copy(0, t).wait()
                block_copy(1, t).wait()

            @pl.when(t > 0)
            def _():
                pltpu.make_async_copy(v_slot.at[t], v_slot.at[t], recv_sem.at[t]).wait()

            for k in range(STEPS_MAX):
                v_old = (v_slot.at[t] if k == 0 else v_f)[...]
                v_half = v_old.astype(bf16)

                def pick(new, old):
                    if k == 0:
                        return new
                    return jnp.where(jnp.full(new.shape, count, jnp.int32) > k, new, old)

                grad_v = jnp.zeros((items, rank), f32)
                for s in starts:
                    rows = pl.ds(s, CHUNK)
                    u_half = u_b[rows, :]
                    approx = lax.dot_general(u_half, v_half, (((1,), (1,)), ((), ())), preferred_element_type=f32)
                    err = jnp.where(m_buf[q, rows, :] != 0, approx - r_buf[q, rows, :], 0.0).astype(bf16)
                    e_b[rows, :] = err
                    grad_v += lax.dot_general(err, u_half, (((0,), (0,)), ((), ())), preferred_element_type=f32)
                v_new = pick(keep * v_old - step_size * grad_v, v_old)
                if k < STEPS_MAX - 1:
                    v_f[...] = v_new
                else:
                    v_send[t] = v_new
                    hop_copy(t).start()

                for s in starts:
                    rows = pl.ds(s, CHUNK)
                    grad_u = jnp.dot(e_b[rows, :], v_half, preferred_element_type=f32)
                    u_old = u_f[rows, :]
                    u_new = pick(keep * u_old - step_size * grad_u, u_old)
                    u_f[rows, :] = u_new
                    u_b[rows, :] = u_new.astype(bf16)
            return carry

        lax.fori_loop(0, hops, sub_epoch, 0)
        u_back = pltpu.make_async_copy(u_f, u_out, out_sem.at[0])
        u_back.start()
        pltpu.make_async_copy(v_slot.at[hops], v_slot.at[hops], recv_sem.at[hops]).wait()
        v_back = pltpu.make_async_copy(v_slot.at[hops], v_out, out_sem.at[1])
        v_back.start()
        for t in range(hops):
            hop_copy(t).wait_send()
        u_back.wait()
        v_back.wait()

    return kernel


def solution(mesh):
    n = mesh.shape["shard"]
    row_spec = P(("rep", "shard"), None)
    hops = EPOCHS * n

    def local_run(ratings, obs_mask, step_counts, user_init, item_init):
        users, rank = user_init.shape
        items = item_init.shape[0]
        f32, bf16 = jnp.float32, jnp.bfloat16
        dma = pltpu.SemaphoreType.DMA
        hbm = pl.BlockSpec(memory_space=pl.ANY)
        return pl.pallas_call(
            make_kernel(n, users, items, rank),
            out_shape=(jax.ShapeDtypeStruct((users, rank), f32), jax.ShapeDtypeStruct((items, rank), f32)),
            in_specs=[pl.BlockSpec(memory_space=pltpu.SMEM), hbm, hbm, hbm, hbm],
            out_specs=(hbm, hbm),
            scratch_shapes=[
                pltpu.VMEM((n, users, items), f32),
                pltpu.VMEM((n, users, items), jnp.int32),
                pltpu.VMEM((users, rank), f32),
                pltpu.VMEM((users, rank), bf16),
                pltpu.VMEM((hops + 1, items, rank), f32),
                pltpu.VMEM((hops, items, rank), f32),
                pltpu.VMEM((items, rank), f32),
                pltpu.VMEM((users, items), bf16),
                dma((n,)), dma((n,)), dma, dma((hops + 1,)), dma((hops,)), dma((2,)),
            ],
            compiler_params=pltpu.CompilerParams(collective_id=0, has_side_effects=True),
            name="dsgd",
        )(step_counts, ratings, obs_mask, user_init, item_init)

    return jax.shard_map(local_run, mesh=mesh, in_specs=(row_spec,) * 5, out_specs=(row_spec, row_spec), check_vma=False)
```

time: 105 us -> 42.3 us (0.40)
  the two profiles are of different devices: /device:TPU:7 before, /device:TPU:0 now
where the time goes in v1:
time: 42.3 us; the launch traced here: 42.1 us
  Pallas kernels  38.8 us (92%)
  local copies, waits for them, and re-layouts  2.66 us (6%)
  between operations  0.65 us (2%)
    pallas_call x1, Pallas kernels, local_run(): pl.pallas_call(make_kernel(n, users, items, rank), out_shape=(jax.ShapeDt...  38.8 us
    unnamed x4, local copies, waits for them, and re-layouts  2.66 us

profile of v1, /device:TPU:0, one launch (start us, length us, event | category | flops | bytes accessed | tf_op | source)
XLA Modules:
  0.0 42.1 jit_solution(14365147922394873569)
XLA Ops:
  0.6 38.8 %dsgd.1 = (f32[640,256]{1,0:T(8,128)}, f32[128,256]{1,0:T(8,128)}) custom-call(s32[1,4]{1,0:T(1,128)} %cnt.1, f32[640,512]{1,0:T(8,128)} %r_hbm.1, s32[640,512]{1,0:T(8,128)} %m_hbm.1, f32[640,256]{1,0:T(8,128)} %u_hbm.1, f32[128,256]{1,0:T(8,128)} %v_hbm.1), custom_call_target="tpu_custom_call" | custom-call | tf_op jit(solution)/shard_map/dsgd/pallas_call | solution.py:127
  39.5 0.0 copy-start
  39.5 2.0 %copy.9 = f32[640,256]{1,0:T(8,128)} copy(f32[640,256]{1,0:T(8,128)} %get-tuple-element.4) | data formatting | bytes 1310720
  41.5 0.0 copy-done
  41.5 0.7 %copy.10 = f32[128,256]{1,0:T(8,128)} copy(f32[128,256]{1,0:T(8,128)S(1)} %copy-done) | data formatting | bytes 262144
Async XLA Ops:
  39.5 2.0 %copy-start = (f32[128,256]{1,0:T(8,128)S(1)}, f32[128,256]{1,0:T(8,128)}, u32[]{:S(2)}) copy-start(f32[128,256]{1,0:T(8,128)} %get-tuple-element.5) | copy-start | bytes 393220

commit v2 on v1

--- a/solution.py
+++ b/solution.py
@@ -19,9 +19,9 @@
     bf16, f32 = jnp.bfloat16, jnp.float32
     starts = range(0, users, CHUNK)
 
-    def kernel(cnt, r_hbm, m_hbm, u_hbm, v_hbm, u_out, v_out,
-               r_buf, m_buf, u_f, u_b, v_slot, v_send, v_f, e_b,
-               r_sem, m_sem, u_sem, recv_sem, send_sem, out_sem):
+    def kernel(cnt_hbm, r_hbm, m_hbm, u_hbm, v_hbm, u_f, v_out,
+               cnt, r_buf, m_buf, u_b, v_slot, v_send, v_f, e_b,
+               r_sem, m_sem, u_sem, cnt_sem, recv_sem, send_sem):
         me = lax.axis_index("shard")
         left, right = lax.rem(me + n - 1, n), lax.rem(me + 1, n)
 
@@ -36,8 +36,10 @@
 
         u_in = pltpu.make_async_copy(u_hbm, u_f, u_sem)
         v_in = pltpu.make_async_copy(v_hbm, v_slot.at[0], recv_sem.at[0])
+        cnt_in = pltpu.make_async_copy(cnt_hbm, cnt, cnt_sem)
         u_in.start()
         v_in.start()
+        cnt_in.start()
         for q in range(n):
             block_copy(0, q).start()
             block_copy(1, q).start()
@@ -45,6 +47,7 @@
         for s in starts:
             u_b[pl.ds(s, CHUNK), :] = u_f[pl.ds(s, CHUNK), :].astype(bf16)
         v_in.wait()
+        cnt_in.wait()
         pl.semaphore_wait(barrier, 2)
 
         def hop_copy(t):
@@ -100,15 +103,10 @@
             return carry
 
         lax.fori_loop(0, hops, sub_epoch, 0)
-        u_back = pltpu.make_async_copy(u_f, u_out, out_sem.at[0])
-        u_back.start()
         pltpu.make_async_copy(v_slot.at[hops], v_slot.at[hops], recv_sem.at[hops]).wait()
-        v_back = pltpu.make_async_copy(v_slot.at[hops], v_out, out_sem.at[1])
-        v_back.start()
+        v_out[...] = v_slot[hops]
         for t in range(hops):
             hop_copy(t).wait_send()
-        u_back.wait()
-        v_back.wait()
 
     return kernel
 
@@ -124,21 +122,22 @@
         f32, bf16 = jnp.float32, jnp.bfloat16
         dma = pltpu.SemaphoreType.DMA
         hbm = pl.BlockSpec(memory_space=pl.ANY)
+        vmem = pl.BlockSpec(memory_space=pltpu.VMEM)
         return pl.pallas_call(
             make_kernel(n, users, items, rank),
-            out_shape=(jax.ShapeDtypeStruct((users, rank), f32), jax.ShapeDtypeStruct((items, rank), f32)),
-            in_specs=[pl.BlockSpec(memory_space=pltpu.SMEM), hbm, hbm, hbm, hbm],
-            out_specs=(hbm, hbm),
+            out_shape=(pltpu.VMEM((users, rank), f32), pltpu.VMEM((items, rank), f32)),
+            in_specs=[hbm, hbm, hbm, hbm, hbm],
+            out_specs=(vmem, vmem),
             scratch_shapes=[
+                pltpu.SMEM((1, n), jnp.int32),
                 pltpu.VMEM((n, users, items), f32),
                 pltpu.VMEM((n, users, items), jnp.int32),
-                pltpu.VMEM((users, rank), f32),
                 pltpu.VMEM((users, rank), bf16),
                 pltpu.VMEM((hops + 1, items, rank), f32),
                 pltpu.VMEM((hops, items, rank), f32),
                 pltpu.VMEM((items, rank), f32),
                 pltpu.VMEM((users, items), bf16),
-                dma((n,)), dma((n,)), dma, dma((hops + 1,)), dma((hops,)), dma((2,)),
+                dma((n,)), dma((n,)), dma, dma, dma((hops + 1,)), dma((hops,)),
             ],
             compiler_params=pltpu.CompilerParams(collective_id=0, has_side_effects=True),
             name="dsgd",

time: 42.3 us -> 39.8 us (0.941)
  Pallas kernels: 38.8 us -> 37.5 us
  local copies, waits for them, and re-layouts: 2.66 us -> 1.49 us
    pallas_call x1, Pallas kernels: 38.8 us -> 37.5 us  [local_run(): pl.pallas_call(make_kernel(n, users, items, rank), out_shape=(pltpu.VMEM(...]
    unnamed x4 -> x2, local copies, waits for them, and re-layouts: 2.66 us -> 1.49 us
where the time goes in v2:
time: 39.8 us; the launch traced here: 39.7 us
  Pallas kernels  37.5 us (94%)
  local copies, waits for them, and re-layouts  1.49 us (4%)
  between operations  0.64 us (2%)
    pallas_call x1, Pallas kernels, local_run(): pl.pallas_call(make_kernel(n, users, items, rank), out_shape=(pltpu.VMEM(...  37.5 us
    unnamed x2, local copies, waits for them, and re-layouts  1.49 us

profile of v2, /device:TPU:0, one launch (start us, length us, event | category | flops | bytes accessed | tf_op | source)
XLA Modules:
  0.0 39.7 jit_solution(7779238315296051970)
XLA Ops:
  0.6 37.5 %dsgd.1 = (f32[640,256]{1,0:T(8,128)S(1)}, f32[128,256]{1,0:T(8,128)S(1)}) custom-call(s32[1,4]{1,0:T(1,128)} %cnt_hbm.1, f32[640,512]{1,0:T(8,128)} %r_hbm.1, s32[640,512]{1,0:T(8,128)} %m_hbm.1, f32[640,256]{1,0:T(8,128)} %u_hbm.1, f32[128,256]{1,0:T(8,128)} %v_hbm.1), custom_call_target="tpu_custom_call" | custom-call | tf_op jit(solution)/shard_map/dsgd/pallas_call | solution.py:126
  38.2 0.8 %copy.9 = f32[640,256]{1,0:T(8,128)} copy(f32[640,256]{1,0:T(8,128)S(1)} %get-tuple-element.2) | data formatting | bytes 1310720
  39.0 0.7 %copy.10 = f32[128,256]{1,0:T(8,128)} copy(f32[128,256]{1,0:T(8,128)S(1)} %get-tuple-element.3) | data formatting | bytes 262144

commit v3 on v2

--- a/solution.py
+++ b/solution.py
@@ -8,7 +8,7 @@
 
 EPOCHS = 2
 STEPS_MAX = 4
-CHUNK = 128
+CHUNK = 320
 
 
 def make_kernel(n, users, items, rank):

time: 39.8 us -> 40.8 us (1.025)
  Pallas kernels: 37.5 us -> 38.6 us
    pallas_call x1, Pallas kernels: 37.5 us -> 38.6 us  [local_run(): pl.pallas_call(make_kernel(n, users, items, rank), out_shape=(pltpu.VMEM(...]
where the time goes in v3:
time: 40.8 us; the launch traced here: 40.7 us
  Pallas kernels  38.6 us (95%)
  local copies, waits for them, and re-layouts  1.49 us (4%)
  between operations  0.64 us (2%)
    pallas_call x1, Pallas kernels, local_run(): pl.pallas_call(make_kernel(n, users, items, rank), out_shape=(pltpu.VMEM(...  38.6 us
    unnamed x2, local copies, waits for them, and re-layouts  1.49 us

profile of v3, /device:TPU:0, one launch (start us, length us, event | category | flops | bytes accessed | tf_op | source)
XLA Modules:
  0.0 40.7 jit_solution(4022159497086114599)
XLA Ops:
  0.6 38.6 %dsgd.1 = (f32[640,256]{1,0:T(8,128)S(1)}, f32[128,256]{1,0:T(8,128)S(1)}) custom-call(s32[1,4]{1,0:T(1,128)} %cnt_hbm.1, f32[640,512]{1,0:T(8,128)} %r_hbm.1, s32[640,512]{1,0:T(8,128)} %m_hbm.1, f32[640,256]{1,0:T(8,128)} %u_hbm.1, f32[128,256]{1,0:T(8,128)} %v_hbm.1), custom_call_target="tpu_custom_call" | custom-call | tf_op jit(solution)/shard_map/dsgd/pallas_call | solution.py:126
  39.2 0.8 %copy.9 = f32[640,256]{1,0:T(8,128)} copy(f32[640,256]{1,0:T(8,128)S(1)} %get-tuple-element.2) | data formatting | bytes 1310720
  40.1 0.7 %copy.10 = f32[128,256]{1,0:T(8,128)} copy(f32[128,256]{1,0:T(8,128)S(1)} %get-tuple-element.3) | data formatting | bytes 262144

commit v4 on v3

--- a/solution.py
+++ b/solution.py
@@ -8,7 +8,7 @@
 
 EPOCHS = 2
 STEPS_MAX = 4
-CHUNK = 320
+TILE = 256
 
 
 def make_kernel(n, users, items, rank):
@@ -17,10 +17,19 @@
     keep = 1.0 - step_size * decay
     hops = EPOCHS * n
     bf16, f32 = jnp.bfloat16, jnp.float32
-    starts = range(0, users, CHUNK)
+    tiles = [(s, min(TILE, users - s)) for s in range(0, users, TILE)]
 
-    def kernel(cnt_hbm, r_hbm, m_hbm, u_hbm, v_hbm, u_f, v_out,
-               cnt, r_buf, m_buf, u_b, v_slot, v_send, v_f, e_b,
+    def nn(a, b):
+        return lax.dot_general(a, b, (((1,), (0,)), ((), ())), preferred_element_type=f32)
+
+    def nt(a, b):
+        return lax.dot_general(a, b, (((1,), (1,)), ((), ())), preferred_element_type=f32)
+
+    def split(w, rows):
+        return [(0, rows)] if w == TILE else [(0, rows // 2), (rows // 2, rows // 2)]
+
+    def kernel(cnt_hbm, r_hbm, m_hbm, u_hbm, v_hbm, u_out, v_out,
+               cnt, r_buf, m_buf, r_t, m_t, ut_f, ut_b, v_slot, v_send, v_f, e_b, vt_b,
                r_sem, m_sem, u_sem, cnt_sem, recv_sem, send_sem):
         me = lax.axis_index("shard")
         left, right = lax.rem(me + n - 1, n), lax.rem(me + 1, n)
@@ -34,7 +43,7 @@
             col = pl.multiple_of(lax.rem(me + q, n) * items, items)
             return pltpu.make_async_copy(src.at[:, pl.ds(col, items)], dst.at[q], sem.at[q])
 
-        u_in = pltpu.make_async_copy(u_hbm, u_f, u_sem)
+        u_in = pltpu.make_async_copy(u_hbm, u_out, u_sem)
         v_in = pltpu.make_async_copy(v_hbm, v_slot.at[0], recv_sem.at[0])
         cnt_in = pltpu.make_async_copy(cnt_hbm, cnt, cnt_sem)
         u_in.start()
@@ -43,9 +52,20 @@
         for q in range(n):
             block_copy(0, q).start()
             block_copy(1, q).start()
+
+        def flip_block(q):
+            block_copy(0, q).wait()
+            block_copy(1, q).wait()
+            for s in range(0, users, 128):
+                r_t[q, :, pl.ds(s, 128)] = r_buf[q, pl.ds(s, 128), :].T
+                m_t[q, :, pl.ds(s, 128)] = m_buf[q, pl.ds(s, 128), :].astype(f32).T.astype(bf16)
+
         u_in.wait()
-        for s in starts:
-            u_b[pl.ds(s, CHUNK), :] = u_f[pl.ds(s, CHUNK), :].astype(bf16)
+        for s in range(0, users, 128):
+            flipped = u_out[pl.ds(s, 128), :].T
+            ut_f[:, pl.ds(s, 128)] = flipped
+            ut_b[:, pl.ds(s, 128)] = flipped.astype(bf16)
+        flip_block(0)
         v_in.wait()
         cnt_in.wait()
         pl.semaphore_wait(barrier, 2)
@@ -60,11 +80,6 @@
             q = lax.rem(t, n)
             count = cnt[0, lax.rem(me + t, n)]
 
-            @pl.when(t < n)
-            def _():
-                block_copy(0, t).wait()
-                block_copy(1, t).wait()
-
             @pl.when(t > 0)
             def _():
                 pltpu.make_async_copy(v_slot.at[t], v_slot.at[t], recv_sem.at[t]).wait()
@@ -72,37 +87,57 @@
             for k in range(STEPS_MAX):
                 v_old = (v_slot.at[t] if k == 0 else v_f)[...]
                 v_half = v_old.astype(bf16)
+                vt_b[...] = v_half.T
 
                 def pick(new, old):
                     if k == 0:
                         return new
                     return jnp.where(jnp.full(new.shape, count, jnp.int32) > k, new, old)
 
-                grad_v = jnp.zeros((items, rank), f32)
-                for s in starts:
-                    rows = pl.ds(s, CHUNK)
-                    u_half = u_b[rows, :]
-                    approx = lax.dot_general(u_half, v_half, (((1,), (1,)), ((), ())), preferred_element_type=f32)
-                    err = jnp.where(m_buf[q, rows, :] != 0, approx - r_buf[q, rows, :], 0.0).astype(bf16)
-                    e_b[rows, :] = err
-                    grad_v += lax.dot_general(err, u_half, (((0,), (0,)), ((), ())), preferred_element_type=f32)
-                v_new = pick(keep * v_old - step_size * grad_v, v_old)
+                for s, w in tiles:
+                    cols = pl.ds(s, w)
+                    for a, h in split(w, items):
+                        approx = nn(v_half[a:a + h], ut_b[:, cols])
+                        err = (approx - r_t[q, pl.ds(a, h), cols]).astype(bf16)
+                        seen = m_t[q, pl.ds(a, h), cols] != 0
+                        e_b[pl.ds(a, h), cols] = jnp.where(seen, err, jnp.zeros_like(err))
+                halves = []
+                for a, h in ((0, items // 2), (items // 2, items // 2)):
+                    halves.append(keep * v_old[a:a + h])
+                for s, w in tiles:
+                    cols = pl.ds(s, w)
+                    if w == TILE:
+                        g = step_size * nt(e_b[:, cols], ut_b[:, cols])
+                        halves = [halves[0] - g[:items // 2], halves[1] - g[items // 2:]]
+                    else:
+                        halves = [x - step_size * nt(e_b[pl.ds(i * items // 2, items // 2), cols], ut_b[:, cols])
+                                  for i, x in enumerate(halves)]
+                v_new = pick(jnp.concatenate(halves, axis=0), v_old)
                 if k < STEPS_MAX - 1:
                     v_f[...] = v_new
                 else:
                     v_send[t] = v_new
                     hop_copy(t).start()
 
-                for s in starts:
-                    rows = pl.ds(s, CHUNK)
-                    grad_u = jnp.dot(e_b[rows, :], v_half, preferred_element_type=f32)
-                    u_old = u_f[rows, :]
-                    u_new = pick(keep * u_old - step_size * grad_u, u_old)
-                    u_f[rows, :] = u_new
-                    u_b[rows, :] = u_new.astype(bf16)
+                for s, w in tiles:
+                    cols = pl.ds(s, w)
+                    for a, h in split(w, rank):
+                        rows = pl.ds(a, h)
+                        grad = nn(vt_b[rows, :], e_b[:, cols])
+                        u_old = ut_f[rows, cols]
+                        u_new = pick(keep * u_old - step_size * grad, u_old)
+                        ut_f[rows, cols] = u_new
+                        ut_b[rows, cols] = u_new.astype(bf16)
+
+            @pl.when(t + 1 < n)
+            def _():
+                flip_block(t + 1)
+
             return carry
 
         lax.fori_loop(0, hops, sub_epoch, 0)
+        for s in range(0, users, 128):
+            u_out[pl.ds(s, 128), :] = ut_f[:, pl.ds(s, 128)].T
         pltpu.make_async_copy(v_slot.at[hops], v_slot.at[hops], recv_sem.at[hops]).wait()
         v_out[...] = v_slot[hops]
         for t in range(hops):
@@ -132,11 +167,15 @@
                 pltpu.SMEM((1, n), jnp.int32),
                 pltpu.VMEM((n, users, items), f32),
                 pltpu.VMEM((n, users, items), jnp.int32),
-                pltpu.VMEM((users, rank), bf16),
+                pltpu.VMEM((n, items, users), f32),
+                pltpu.VMEM((n, items, users), bf16),
+                pltpu.VMEM((rank, users), f32),
+                pltpu.VMEM((rank, users), bf16),
                 pltpu.VMEM((hops + 1, items, rank), f32),
                 pltpu.VMEM((hops, items, rank), f32),
                 pltpu.VMEM((items, rank), f32),
-                pltpu.VMEM((users, items), bf16),
+                pltpu.VMEM((items, users), bf16),
+                pltpu.VMEM((rank, items), bf16),
                 dma((n,)), dma((n,)), dma, dma, dma((hops + 1,)), dma((hops,)),
             ],
             compiler_params=pltpu.CompilerParams(collective_id=0, has_side_effects=True),

time: 40.8 us -> 37.1 us (0.909)
  Pallas kernels: 38.6 us -> 34.8 us
    pallas_call x1, Pallas kernels: 38.6 us -> 34.8 us  [local_run(): pl.pallas_call(make_kernel(n, users, items, rank), out_shape=(pltpu.VMEM(...]
where the time goes in v4:
time: 37.1 us; the launch traced here: 37 us
  Pallas kernels  34.8 us (94%)
  local copies, waits for them, and re-layouts  1.49 us (4%)
  between operations  0.64 us (2%)
    pallas_call x1, Pallas kernels, local_run(): pl.pallas_call(make_kernel(n, users, items, rank), out_shape=(pltpu.VMEM(...  34.8 us
    unnamed x2, local copies, waits for them, and re-layouts  1.49 us

profile of v4, /device:TPU:0, one launch (start us, length us, event | category | flops | bytes accessed | tf_op | source)
XLA Modules:
  0.0 37.0 jit_solution(11093538650014287254)
XLA Ops:
  0.6 34.8 %dsgd.1 = (f32[640,256]{1,0:T(8,128)S(1)}, f32[128,256]{1,0:T(8,128)S(1)}) custom-call(s32[1,4]{1,0:T(1,128)} %cnt_hbm.1, f32[640,512]{1,0:T(8,128)} %r_hbm.1, s32[640,512]{1,0:T(8,128)} %m_hbm.1, f32[640,256]{1,0:T(8,128)} %u_hbm.1, f32[128,256]{1,0:T(8,128)} %v_hbm.1), custom_call_target="tpu_custom_call" | custom-call | tf_op jit(solution)/shard_map/dsgd/pallas_call | solution.py:161
  35.5 0.8 %copy.9 = f32[640,256]{1,0:T(8,128)} copy(f32[640,256]{1,0:T(8,128)S(1)} %get-tuple-element.2) | data formatting | bytes 1310720
  36.3 0.7 %copy.10 = f32[128,256]{1,0:T(8,128)} copy(f32[128,256]{1,0:T(8,128)S(1)} %get-tuple-element.3) | data formatting | bytes 262144

commit v5 on v4

--- a/solution.py
+++ b/solution.py
@@ -49,9 +49,8 @@
         u_in.start()
         v_in.start()
         cnt_in.start()
-        for q in range(n):
-            block_copy(0, q).start()
-            block_copy(1, q).start()
+        block_copy(0, 0).start()
+        block_copy(1, 0).start()
 
         def flip_block(q):
             block_copy(0, q).wait()
@@ -66,6 +65,9 @@
             ut_f[:, pl.ds(s, 128)] = flipped
             ut_b[:, pl.ds(s, 128)] = flipped.astype(bf16)
         flip_block(0)
+        for q in range(1, n):
+            block_copy(0, q).start()
+            block_copy(1, q).start()
         v_in.wait()
         cnt_in.wait()
         pl.semaphore_wait(barrier, 2)
@@ -87,7 +89,15 @@
             for k in range(STEPS_MAX):
                 v_old = (v_slot.at[t] if k == 0 else v_f)[...]
                 v_half = v_old.astype(bf16)
-                vt_b[...] = v_half.T
+                if k == 0:
+                    limit, keep_k = 0.5, keep
+                    vt_b[...] = v_half.T
+                else:
+                    live = count > k
+                    limit = jnp.where(live, 0.5, 2.0)
+                    keep_k = jnp.where(live, keep, 1.0)
+                    v_live = jnp.where(jnp.full(v_half.shape, count, jnp.int32) > k, v_old, 0.0).astype(bf16)
+                    vt_b[...] = v_live.T
 
                 def pick(new, old):
                     if k == 0:
@@ -99,35 +109,50 @@
                     for a, h in split(w, items):
                         approx = nn(v_half[a:a + h], ut_b[:, cols])
                         err = (approx - r_t[q, pl.ds(a, h), cols]).astype(bf16)
-                        seen = m_t[q, pl.ds(a, h), cols] != 0
+                        seen = m_t[q, pl.ds(a, h), cols] > jnp.full((h, w), limit, f32).astype(bf16)
                         e_b[pl.ds(a, h), cols] = jnp.where(seen, err, jnp.zeros_like(err))
-                halves = []
-                for a, h in ((0, items // 2), (items // 2, items // 2)):
-                    halves.append(keep * v_old[a:a + h])
-                for s, w in tiles:
+                half = items // 2
+                parts = [keep * v_old[i * half:(i + 1) * half] for i in range(2)]
+
+                def item_grad(s, w):
                     cols = pl.ds(s, w)
                     if w == TILE:
                         g = step_size * nt(e_b[:, cols], ut_b[:, cols])
-                        halves = [halves[0] - g[:items // 2], halves[1] - g[items // 2:]]
+                        for i in range(2):
+                            parts[i] = parts[i] - g[i * half:(i + 1) * half]
                     else:
-                        halves = [x - step_size * nt(e_b[pl.ds(i * items // 2, items // 2), cols], ut_b[:, cols])
-                                  for i, x in enumerate(halves)]
-                v_new = pick(jnp.concatenate(halves, axis=0), v_old)
-                if k < STEPS_MAX - 1:
-                    v_f[...] = v_new
-                else:
-                    v_send[t] = v_new
-                    hop_copy(t).start()
-
-                for s, w in tiles:
+                        for i in range(2):
+                            parts[i] = parts[i] - step_size * nt(e_b[pl.ds(i * half, half), cols], ut_b[:, cols])
+
+                def item_update():
+                    v_new = pick(jnp.concatenate(parts, axis=0), v_old)
+                    if k < STEPS_MAX - 1:
+                        v_f[...] = v_new
+                    else:
+                        v_send[t] = v_new
+                        hop_copy(t).start()
+
+                def user_update(s, w):
                     cols = pl.ds(s, w)
                     for a, h in split(w, rank):
                         rows = pl.ds(a, h)
                         grad = nn(vt_b[rows, :], e_b[:, cols])
-                        u_old = ut_f[rows, cols]
-                        u_new = pick(keep * u_old - step_size * grad, u_old)
+                        u_new = keep_k * ut_f[rows, cols] - step_size * grad
                         ut_f[rows, cols] = u_new
                         ut_b[rows, cols] = u_new.astype(bf16)
+
+                wide = [x for x in tiles if x[1] == TILE]
+                narrow = [x for x in tiles if x[1] < TILE]
+                if k < STEPS_MAX - 1:
+                    order = [(item_grad, wide), (user_update, wide), (item_grad, narrow), (item_update, None), (user_update, narrow)]
+                else:
+                    order = [(item_grad, wide), (item_grad, narrow), (item_update, None), (user_update, wide), (user_update, narrow)]
+                for piece, group in order:
+                    if group is None:
+                        piece()
+                    else:
+                        for x in group:
+                            piece(*x)
 
             @pl.when(t + 1 < n)
             def _():

time: 37.1 us -> 36.1 us (0.973)
  Pallas kernels: 34.8 us -> 33.9 us
    pallas_call x1, Pallas kernels: 34.8 us -> 33.9 us  [local_run(): pl.pallas_call(make_kernel(n, users, items, rank), out_shape=(pltpu.VMEM(...]
where the time goes in v5:
time: 36.1 us; the launch traced here: 36 us
  Pallas kernels  33.9 us (94%)
  local copies, waits for them, and re-layouts  1.49 us (4%)
  between operations  0.64 us (2%)
    pallas_call x1, Pallas kernels, local_run(): pl.pallas_call(make_kernel(n, users, items, rank), out_shape=(pltpu.VMEM(...  33.9 us
    unnamed x2, local copies, waits for them, and re-layouts  1.49 us

profile of v5, /device:TPU:0, one launch (start us, length us, event | category | flops | bytes accessed | tf_op | source)
XLA Modules:
  0.0 36.0 jit_solution(11359232792069562727)
XLA Ops:
  0.6 33.9 %dsgd.1 = (f32[640,256]{1,0:T(8,128)S(1)}, f32[128,256]{1,0:T(8,128)S(1)}) custom-call(s32[1,4]{1,0:T(1,128)} %cnt_hbm.1, f32[640,512]{1,0:T(8,128)} %r_hbm.1, s32[640,512]{1,0:T(8,128)} %m_hbm.1, f32[640,256]{1,0:T(8,128)} %u_hbm.1, f32[128,256]{1,0:T(8,128)} %v_hbm.1), custom_call_target="tpu_custom_call" | custom-call | tf_op jit(solution)/shard_map/dsgd/pallas_call | solution.py:186
  34.5 0.8 %copy.9 = f32[640,256]{1,0:T(8,128)} copy(f32[640,256]{1,0:T(8,128)S(1)} %get-tuple-element.2) | data formatting | bytes 1310720
  35.3 0.7 %copy.10 = f32[128,256]{1,0:T(8,128)} copy(f32[128,256]{1,0:T(8,128)S(1)} %get-tuple-element.3) | data formatting | bytes 262144

commit v6 on v5

--- a/solution.py
+++ b/solution.py
@@ -171,6 +171,14 @@
     return kernel
 
 
+def flush(u_vmem, v_vmem, u_out, v_out, sem):
+    copies = [pltpu.make_async_copy(u_vmem, u_out, sem.at[0]), pltpu.make_async_copy(v_vmem, v_out, sem.at[1])]
+    for copy in copies:
+        copy.start()
+    for copy in copies:
+        copy.wait()
+
+
 def solution(mesh):
     n = mesh.shape["shard"]
     row_spec = P(("rep", "shard"), None)
@@ -183,7 +191,7 @@
         dma = pltpu.SemaphoreType.DMA
         hbm = pl.BlockSpec(memory_space=pl.ANY)
         vmem = pl.BlockSpec(memory_space=pltpu.VMEM)
-        return pl.pallas_call(
+        factors = pl.pallas_call(
             make_kernel(n, users, items, rank),
             out_shape=(pltpu.VMEM((users, rank), f32), pltpu.VMEM((items, rank), f32)),
             in_specs=[hbm, hbm, hbm, hbm, hbm],
@@ -206,5 +214,14 @@
             compiler_params=pltpu.CompilerParams(collective_id=0, has_side_effects=True),
             name="dsgd",
         )(step_counts, ratings, obs_mask, user_init, item_init)
+        return pl.pallas_call(
+            flush,
+            out_shape=(jax.ShapeDtypeStruct((users, rank), f32), jax.ShapeDtypeStruct((items, rank), f32)),
+            in_specs=[vmem, vmem],
+            out_specs=(hbm, hbm),
+            scratch_shapes=[dma((2,))],
+            compiler_params=pltpu.CompilerParams(vmem_limit_bytes=1 << 20),
+            name="flush",
+        )(*(pltpu.with_memory_space_constraint(x, pltpu.VMEM) for x in factors))
 
     return jax.shard_map(local_run, mesh=mesh, in_specs=(row_spec,) * 5, out_specs=(row_spec, row_spec), check_vma=False)

time: 36.1 us -> 35.5 us (0.983)
  local copies, waits for them, and re-layouts: 1.49 us -> 0 us
  Pallas kernels: 33.9 us -> 34.7 us
    unnamed x2 -> x0, local copies, waits for them, and re-layouts: 1.49 us -> none
    pallas_call x0 -> x1, Pallas kernels: none -> 0.89 us  [local_run(): pl.pallas_call(flush, out_shape=(jax.ShapeDtypeStruct((users, rank), f32)...]
where the time goes in v6:
time: 35.5 us; the launch traced here: 35.4 us
  Pallas kernels  34.7 us (98%)
  between operations  0.64 us (2%)
    pallas_call x1, Pallas kernels, local_run(): pl.pallas_call(make_kernel(n, users, items, rank), out_shape=(pltpu.VMEM(...  33.9 us
    pallas_call x1, Pallas kernels, local_run(): pl.pallas_call(flush, out_shape=(jax.ShapeDtypeStruct((users, rank), f32)...  0.89 us

profile of v6, /device:TPU:0, one launch (start us, length us, event | category | flops | bytes accessed | tf_op | source)
XLA Modules:
  0.0 35.4 jit_solution(7092724236662996455)
XLA Ops:
  0.6 33.9 %dsgd.1 = (f32[640,256]{1,0:T(8,128)S(1)}, f32[128,256]{1,0:T(8,128)S(1)}) custom-call(s32[1,4]{1,0:T(1,128)} %cnt_hbm.1, f32[640,512]{1,0:T(8,128)} %r_hbm.1, s32[640,512]{1,0:T(8,128)} %m_hbm.1, f32[640,256]{1,0:T(8,128)} %u_hbm.1, f32[128,256]{1,0:T(8,128)} %v_hbm.1), custom_call_target="tpu_custom_call" | custom-call | tf_op jit(solution)/shard_map/dsgd/pallas_call | solution.py:194
  34.5 0.9 %flush.1 = (f32[640,256]{1,0:T(8,128)}, f32[128,256]{1,0:T(8,128)}) custom-call(f32[640,256]{1,0:T(8,128)S(1)} %get-tuple-element.4.u_vmem, f32[128,256]{1,0:T(8,128)S(1)} %get-tuple-element.5.v_vmem), custom_call_target="tpu_custom_call" | custom-call | tf_op jit(solution)/shard_map/flush/pallas_call | solution.py:217

commit v7 on v6

--- a/solution.py
+++ b/solution.py
@@ -9,6 +9,7 @@
 EPOCHS = 2
 STEPS_MAX = 4
 TILE = 256
+PIECES = 4
 
 
 def make_kernel(n, users, items, rank):
@@ -30,7 +31,7 @@
 
     def kernel(cnt_hbm, r_hbm, m_hbm, u_hbm, v_hbm, u_out, v_out,
                cnt, r_buf, m_buf, r_t, m_t, ut_f, ut_b, v_slot, v_send, v_f, e_b, vt_b,
-               r_sem, m_sem, u_sem, cnt_sem, recv_sem, send_sem):
+               r_sem, m_sem, u_sem, v_sem, cnt_sem, recv_sem, send_sem):
         me = lax.axis_index("shard")
         left, right = lax.rem(me + n - 1, n), lax.rem(me + 1, n)
 
@@ -44,7 +45,7 @@
             return pltpu.make_async_copy(src.at[:, pl.ds(col, items)], dst.at[q], sem.at[q])
 
         u_in = pltpu.make_async_copy(u_hbm, u_out, u_sem)
-        v_in = pltpu.make_async_copy(v_hbm, v_slot.at[0], recv_sem.at[0])
+        v_in = pltpu.make_async_copy(v_hbm, v_slot.at[0], v_sem)
         cnt_in = pltpu.make_async_copy(cnt_hbm, cnt, cnt_sem)
         u_in.start()
         v_in.start()
@@ -72,10 +73,11 @@
         cnt_in.wait()
         pl.semaphore_wait(barrier, 2)
 
-        def hop_copy(t):
+        def hop_copy(t, i):
+            rows = pl.ds(i * (items // PIECES), items // PIECES)
             return pltpu.make_async_remote_copy(
-                src_ref=v_send.at[t], dst_ref=v_slot.at[t + 1],
-                send_sem=send_sem.at[t], recv_sem=recv_sem.at[t + 1],
+                src_ref=v_send.at[t, rows], dst_ref=v_slot.at[t + 1, rows],
+                send_sem=send_sem.at[i, t], recv_sem=recv_sem.at[i, t],
                 device_id={"shard": left}, device_id_type=pl.DeviceIdType.MESH)
 
         def sub_epoch(t, carry):
@@ -84,7 +86,8 @@
 
             @pl.when(t > 0)
             def _():
-                pltpu.make_async_copy(v_slot.at[t], v_slot.at[t], recv_sem.at[t]).wait()
+                for i in range(PIECES):
+                    hop_copy(t - 1, i).wait_recv()
 
             for k in range(STEPS_MAX):
                 v_old = (v_slot.at[t] if k == 0 else v_f)[...]
@@ -129,8 +132,10 @@
                     if k < STEPS_MAX - 1:
                         v_f[...] = v_new
                     else:
-                        v_send[t] = v_new
-                        hop_copy(t).start()
+                        for i in range(PIECES):
+                            rows = items // PIECES
+                            v_send[t, pl.ds(i * rows, rows), :] = v_new[i * rows:(i + 1) * rows]
+                            hop_copy(t, i).start()
 
                 def user_update(s, w):
                     cols = pl.ds(s, w)
@@ -163,10 +168,12 @@
         lax.fori_loop(0, hops, sub_epoch, 0)
         for s in range(0, users, 128):
             u_out[pl.ds(s, 128), :] = ut_f[:, pl.ds(s, 128)].T
-        pltpu.make_async_copy(v_slot.at[hops], v_slot.at[hops], recv_sem.at[hops]).wait()
+        for i in range(PIECES):
+            hop_copy(hops - 1, i).wait_recv()
         v_out[...] = v_slot[hops]
         for t in range(hops):
-            hop_copy(t).wait_send()
+            for i in range(PIECES):
+                hop_copy(t, i).wait_send()
 
     return kernel
 
@@ -209,7 +216,7 @@
                 pltpu.VMEM((items, rank), f32),
                 pltpu.VMEM((items, users), bf16),
                 pltpu.VMEM((rank, items), bf16),
-                dma((n,)), dma((n,)), dma, dma, dma((hops + 1,)), dma((hops,)),
+                dma((n,)), dma((n,)), dma, dma, dma, dma((PIECES, hops)), dma((PIECES, hops)),
             ],
             compiler_params=pltpu.CompilerParams(collective_id=0, has_side_effects=True),
             name="dsgd",

time: 35.5 us -> 35.9 us (1.011)
  Pallas kernels: 34.7 us -> 35.2 us
    pallas_call x1, Pallas kernels: 33.9 us -> 34.3 us  [local_run(): pl.pallas_call(make_kernel(n, users, items, rank), out_shape=(pltpu.VMEM(...]
where the time goes in v7:
time: 35.9 us; the launch traced here: 35.8 us
  Pallas kernels  35.2 us (98%)
  between operations  0.64 us (2%)
    pallas_call x1, Pallas kernels, local_run(): pl.pallas_call(make_kernel(n, users, items, rank), out_shape=(pltpu.VMEM(...  34.3 us
    pallas_call x1, Pallas kernels, local_run(): pl.pallas_call(flush, out_shape=(jax.ShapeDtypeStruct((users, rank), f32)...  0.89 us

profile of v7, /device:TPU:0, one launch (start us, length us, event | category | flops | bytes accessed | tf_op | source)
XLA Modules:
  0.0 35.8 jit_solution(563742232213105387)
XLA Ops:
  0.6 34.3 %dsgd.1 = (f32[640,256]{1,0:T(8,128)S(1)}, f32[128,256]{1,0:T(8,128)S(1)}) custom-call(s32[1,4]{1,0:T(1,128)} %cnt_hbm.1, f32[640,512]{1,0:T(8,128)} %r_hbm.1, s32[640,512]{1,0:T(8,128)} %m_hbm.1, f32[640,256]{1,0:T(8,128)} %u_hbm.1, f32[128,256]{1,0:T(8,128)} %v_hbm.1), custom_call_target="tpu_custom_call" | custom-call | tf_op jit(solution)/shard_map/dsgd/pallas_call | solution.py:201
  34.9 0.9 %flush.1 = (f32[640,256]{1,0:T(8,128)}, f32[128,256]{1,0:T(8,128)}) custom-call(f32[640,256]{1,0:T(8,128)S(1)} %get-tuple-element.4.u_vmem, f32[128,256]{1,0:T(8,128)S(1)} %get-tuple-element.5.v_vmem), custom_call_target="tpu_custom_call" | custom-call | tf_op jit(solution)/shard_map/flush/pallas_call | solution.py:224

commit v8 on v6

--- a/solution.py
+++ b/solution.py
@@ -30,7 +30,7 @@
 
     def kernel(cnt_hbm, r_hbm, m_hbm, u_hbm, v_hbm, u_out, v_out,
                cnt, r_buf, m_buf, r_t, m_t, ut_f, ut_b, v_slot, v_send, v_f, e_b, vt_b,
-               r_sem, m_sem, u_sem, cnt_sem, recv_sem, send_sem):
+               blk_sem, u_sem, v_sem, cnt_sem, recv_sem, send_sem):
         me = lax.axis_index("shard")
         left, right = lax.rem(me + n - 1, n), lax.rem(me + 1, n)
 
@@ -39,32 +39,38 @@
             pl.semaphore_signal(barrier, inc=1, device_id={"shard": peer}, device_id_type=pl.DeviceIdType.MESH)
 
         def block_copy(kind, q):
-            src, dst, sem = ((r_hbm, r_buf, r_sem), (m_hbm, m_buf, m_sem))[kind]
+            src, dst = ((r_hbm, r_buf), (m_hbm, m_buf))[kind]
             col = pl.multiple_of(lax.rem(me + q, n) * items, items)
-            return pltpu.make_async_copy(src.at[:, pl.ds(col, items)], dst.at[q], sem.at[q])
+            return pltpu.make_async_copy(src.at[:, pl.ds(col, items)], dst.at[q], blk_sem.at[kind, min(q, 1)])
+
+        def block_wait(first, count):
+            for kind, buf in enumerate((r_buf, m_buf)):
+                blocks = buf.at[pl.ds(first, count)]
+                pltpu.make_async_copy(blocks, blocks, blk_sem.at[kind, min(first, 1)]).wait()
 
         u_in = pltpu.make_async_copy(u_hbm, u_out, u_sem)
-        v_in = pltpu.make_async_copy(v_hbm, v_slot.at[0], recv_sem.at[0])
+        v_in = pltpu.make_async_copy(v_hbm, v_slot.at[0], v_sem)
         cnt_in = pltpu.make_async_copy(cnt_hbm, cnt, cnt_sem)
+        block_copy(0, 0).start()
+        block_copy(1, 0).start()
         u_in.start()
         v_in.start()
         cnt_in.start()
-        block_copy(0, 0).start()
-        block_copy(1, 0).start()
 
         def flip_block(q):
-            block_copy(0, q).wait()
-            block_copy(1, q).wait()
             for s in range(0, users, 128):
-                r_t[q, :, pl.ds(s, 128)] = r_buf[q, pl.ds(s, 128), :].T
-                m_t[q, :, pl.ds(s, 128)] = m_buf[q, pl.ds(s, 128), :].astype(f32).T.astype(bf16)
-
+                rows, cols = pl.ds(s, 128), pl.ds(s, 128)
+                marked = jnp.where(m_buf[q, rows, :] != 0, r_buf[q, rows, :], jnp.nan).T
+                r_t[q, :, cols] = marked
+                m_t[q, :, cols] = jnp.where(marked == marked, 1.0, 0.0).astype(bf16)
+
+        block_wait(0, 1)
+        flip_block(0)
         u_in.wait()
         for s in range(0, users, 128):
             flipped = u_out[pl.ds(s, 128), :].T
             ut_f[:, pl.ds(s, 128)] = flipped
             ut_b[:, pl.ds(s, 128)] = flipped.astype(bf16)
-        flip_block(0)
         for q in range(1, n):
             block_copy(0, q).start()
             block_copy(1, q).start()
@@ -72,10 +78,10 @@
         cnt_in.wait()
         pl.semaphore_wait(barrier, 2)
 
-        def hop_copy(t):
+        def hop_copy(t, last=False):
             return pltpu.make_async_remote_copy(
-                src_ref=v_send.at[t], dst_ref=v_slot.at[t + 1],
-                send_sem=send_sem.at[t], recv_sem=recv_sem.at[t + 1],
+                src_ref=v_send.at[lax.rem(t, 2)], dst_ref=v_out if last else v_slot.at[t + 1],
+                send_sem=send_sem.at[lax.rem(t, 2)], recv_sem=recv_sem.at[lax.rem(t, n)],
                 device_id={"shard": left}, device_id_type=pl.DeviceIdType.MESH)
 
         def sub_epoch(t, carry):
@@ -84,7 +90,7 @@
 
             @pl.when(t > 0)
             def _():
-                pltpu.make_async_copy(v_slot.at[t], v_slot.at[t], recv_sem.at[t]).wait()
+                hop_copy(t - 1).wait_recv()
 
             for k in range(STEPS_MAX):
                 v_old = (v_slot.at[t] if k == 0 else v_f)[...]
@@ -129,8 +135,15 @@
                     if k < STEPS_MAX - 1:
                         v_f[...] = v_new
                     else:
-                        v_send[t] = v_new
-                        hop_copy(t).start()
+                        v_send[lax.rem(t, 2)] = v_new
+
+                        @pl.when(t < hops - 1)
+                        def _():
+                            hop_copy(t).start()
+
+                        @pl.when(t == hops - 1)
+                        def _():
+                            hop_copy(t, last=True).start()
 
                 def user_update(s, w):
                     cols = pl.ds(s, w)
@@ -154,19 +167,25 @@
                         for x in group:
                             piece(*x)
 
+            @pl.when(t == 0)
+            def _():
+                block_wait(1, n - 1)
+
             @pl.when(t + 1 < n)
             def _():
                 flip_block(t + 1)
+
+            @pl.when(t > 0)
+            def _():
+                hop_copy(t - 1).wait_send()
 
             return carry
 
         lax.fori_loop(0, hops, sub_epoch, 0)
         for s in range(0, users, 128):
             u_out[pl.ds(s, 128), :] = ut_f[:, pl.ds(s, 128)].T
-        pltpu.make_async_copy(v_slot.at[hops], v_slot.at[hops], recv_sem.at[hops]).wait()
-        v_out[...] = v_slot[hops]
-        for t in range(hops):
-            hop_copy(t).wait_send()
+        hop_copy(hops - 1, last=True).wait_recv()
+        hop_copy(hops - 1, last=True).wait_send()
 
     return kernel
 
@@ -204,12 +223,12 @@
                 pltpu.VMEM((n, items, users), bf16),
                 pltpu.VMEM((rank, users), f32),
                 pltpu.VMEM((rank, users), bf16),
-                pltpu.VMEM((hops + 1, items, rank), f32),
                 pltpu.VMEM((hops, items, rank), f32),
+                pltpu.VMEM((2, items, rank), f32),
                 pltpu.VMEM((items, rank), f32),
                 pltpu.VMEM((items, users), bf16),
                 pltpu.VMEM((rank, items), bf16),
-                dma((n,)), dma((n,)), dma, dma, dma((hops + 1,)), dma((hops,)),
+                dma((2, 2)), dma, dma, dma, dma((n,)), dma((2,)),
             ],
             compiler_params=pltpu.CompilerParams(collective_id=0, has_side_effects=True),
             name="dsgd",

time: 35.5 us -> 35.4 us (level)
  no operation moved by 1% of the time
where the time goes in v8:
time: 35.4 us; the launch traced here: 35.2 us
  Pallas kernels  34.6 us (98%)
  between operations  0.64 us (2%)
    pallas_call x1, Pallas kernels, local_run(): pl.pallas_call(make_kernel(n, users, items, rank), out_shape=(pltpu.VMEM(...  33.7 us
    pallas_call x1, Pallas kernels, local_run(): pl.pallas_call(flush, out_shape=(jax.ShapeDtypeStruct((users, rank), f32)...  0.89 us

profile of v8, /device:TPU:0, one launch (start us, length us, event | category | flops | bytes accessed | tf_op | source)
XLA Modules:
  0.0 35.2 jit_solution(1604814630465417257)
XLA Ops:
  0.6 33.7 %dsgd.1 = (f32[640,256]{1,0:T(8,128)S(1)}, f32[128,256]{1,0:T(8,128)S(1)}) custom-call(s32[1,4]{1,0:T(1,128)} %cnt_hbm.1, f32[640,512]{1,0:T(8,128)} %r_hbm.1, s32[640,512]{1,0:T(8,128)} %m_hbm.1, f32[640,256]{1,0:T(8,128)} %u_hbm.1, f32[128,256]{1,0:T(8,128)} %v_hbm.1), custom_call_target="tpu_custom_call" | custom-call | tf_op jit(solution)/shard_map/dsgd/pallas_call | solution.py:213
  34.3 0.9 %flush.1 = (f32[640,256]{1,0:T(8,128)}, f32[128,256]{1,0:T(8,128)}) custom-call(f32[640,256]{1,0:T(8,128)S(1)} %get-tuple-element.4.u_vmem, f32[128,256]{1,0:T(8,128)S(1)} %get-tuple-element.5.v_vmem), custom_call_target="tpu_custom_call" | custom-call | tf_op jit(solution)/shard_map/flush/pallas_call | solution.py:236

commit v9 on v8

--- a/solution.py
+++ b/solution.py
@@ -51,9 +51,9 @@
         u_in = pltpu.make_async_copy(u_hbm, u_out, u_sem)
         v_in = pltpu.make_async_copy(v_hbm, v_slot.at[0], v_sem)
         cnt_in = pltpu.make_async_copy(cnt_hbm, cnt, cnt_sem)
+        u_in.start()
         block_copy(0, 0).start()
         block_copy(1, 0).start()
-        u_in.start()
         v_in.start()
         cnt_in.start()
 
@@ -64,16 +64,16 @@
                 r_t[q, :, cols] = marked
                 m_t[q, :, cols] = jnp.where(marked == marked, 1.0, 0.0).astype(bf16)
 
-        block_wait(0, 1)
-        flip_block(0)
         u_in.wait()
         for s in range(0, users, 128):
             flipped = u_out[pl.ds(s, 128), :].T
             ut_f[:, pl.ds(s, 128)] = flipped
             ut_b[:, pl.ds(s, 128)] = flipped.astype(bf16)
+        block_wait(0, 1)
         for q in range(1, n):
             block_copy(0, q).start()
             block_copy(1, q).start()
+        flip_block(0)
         v_in.wait()
         cnt_in.wait()
         pl.semaphore_wait(barrier, 2)

time: 35.4 us -> 35.4 us (level)
  no operation moved by 1% of the time
where the time goes in v9:
time: 35.4 us; the launch traced here: 35.2 us
  Pallas kernels  34.6 us (98%)
  between operations  0.64 us (2%)
    pallas_call x1, Pallas kernels, local_run(): pl.pallas_call(make_kernel(n, users, items, rank), out_shape=(pltpu.VMEM(...  33.7 us
    pallas_call x1, Pallas kernels, local_run(): pl.pallas_call(flush, out_shape=(jax.ShapeDtypeStruct((users, rank), f32)...  0.89 us

profile of v9, /device:TPU:0, one launch (start us, length us, event | category | flops | bytes accessed | tf_op | source)
XLA Modules:
  0.0 35.2 jit_solution(5882076487063555262)
XLA Ops:
  0.6 33.7 %dsgd.1 = (f32[640,256]{1,0:T(8,128)S(1)}, f32[128,256]{1,0:T(8,128)S(1)}) custom-call(s32[1,4]{1,0:T(1,128)} %cnt_hbm.1, f32[640,512]{1,0:T(8,128)} %r_hbm.1, s32[640,512]{1,0:T(8,128)} %m_hbm.1, f32[640,256]{1,0:T(8,128)} %u_hbm.1, f32[128,256]{1,0:T(8,128)} %v_hbm.1), custom_call_target="tpu_custom_call" | custom-call | tf_op jit(solution)/shard_map/dsgd/pallas_call | solution.py:213
  34.3 0.9 %flush.1 = (f32[640,256]{1,0:T(8,128)}, f32[128,256]{1,0:T(8,128)}) custom-call(f32[640,256]{1,0:T(8,128)S(1)} %get-tuple-element.4.u_vmem, f32[128,256]{1,0:T(8,128)S(1)} %get-tuple-element.5.v_vmem), custom_call_target="tpu_custom_call" | custom-call | tf_op jit(solution)/shard_map/flush/pallas_call | solution.py:236

commit v10 on v9

--- a/solution.py
+++ b/solution.py
@@ -29,7 +29,7 @@
         return [(0, rows)] if w == TILE else [(0, rows // 2), (rows // 2, rows // 2)]
 
     def kernel(cnt_hbm, r_hbm, m_hbm, u_hbm, v_hbm, u_out, v_out,
-               cnt, r_buf, m_buf, r_t, m_t, ut_f, ut_b, v_slot, v_send, v_f, e_b, vt_b,
+               cnt, r_buf, m_buf, r_t, m_t, ut_f, ut_b, u_b, v_slot, v_send, v_f, e_b, vt_b,
                blk_sem, u_sem, v_sem, cnt_sem, recv_sem, send_sem):
         me = lax.axis_index("shard")
         left, right = lax.rem(me + n - 1, n), lax.rem(me + 1, n)
@@ -69,6 +69,7 @@
             flipped = u_out[pl.ds(s, 128), :].T
             ut_f[:, pl.ds(s, 128)] = flipped
             ut_b[:, pl.ds(s, 128)] = flipped.astype(bf16)
+            u_b[pl.ds(s, 128), :] = u_out[pl.ds(s, 128), :].astype(bf16)
         block_wait(0, 1)
         for q in range(1, n):
             block_copy(0, q).start()
@@ -123,12 +124,12 @@
                 def item_grad(s, w):
                     cols = pl.ds(s, w)
                     if w == TILE:
-                        g = step_size * nt(e_b[:, cols], ut_b[:, cols])
+                        g = step_size * nn(e_b[:, cols], u_b[cols, :])
                         for i in range(2):
                             parts[i] = parts[i] - g[i * half:(i + 1) * half]
                     else:
                         for i in range(2):
-                            parts[i] = parts[i] - step_size * nt(e_b[pl.ds(i * half, half), cols], ut_b[:, cols])
+                            parts[i] = parts[i] - step_size * nn(e_b[pl.ds(i * half, half), cols], u_b[cols, :])
 
                 def item_update():
                     v_new = pick(jnp.concatenate(parts, axis=0), v_old)
@@ -152,7 +153,9 @@
                         grad = nn(vt_b[rows, :], e_b[:, cols])
                         u_new = keep_k * ut_f[rows, cols] - step_size * grad
                         ut_f[rows, cols] = u_new
-                        ut_b[rows, cols] = u_new.astype(bf16)
+                        u_half = u_new.astype(bf16)
+                        ut_b[rows, cols] = u_half
+                        u_b[cols, rows] = u_half.T
 
                 wide = [x for x in tiles if x[1] == TILE]
                 narrow = [x for x in tiles if x[1] < TILE]
@@ -223,6 +226,7 @@
                 pltpu.VMEM((n, items, users), bf16),
                 pltpu.VMEM((rank, users), f32),
                 pltpu.VMEM((rank, users), bf16),
+                pltpu.VMEM((users, rank), bf16),
                 pltpu.VMEM((hops, items, rank), f32),
                 pltpu.VMEM((2, items, rank), f32),
                 pltpu.VMEM((items, rank), f32),

time: 35.4 us -> 35.5 us (level)
  no operation moved by 1% of the time
where the time goes in v10:
time: 35.5 us; the launch traced here: 35.3 us
  Pallas kernels  34.7 us (98%)
  between operations  0.64 us (2%)
    pallas_call x1, Pallas kernels, local_run(): pl.pallas_call(make_kernel(n, users, items, rank), out_shape=(pltpu.VMEM(...  33.8 us
    pallas_call x1, Pallas kernels, local_run(): pl.pallas_call(flush, out_shape=(jax.ShapeDtypeStruct((users, rank), f32)...  0.89 us

profile of v10, /device:TPU:0, one launch (start us, length us, event | category | flops | bytes accessed | tf_op | source)
XLA Modules:
  0.0 35.3 jit_solution(7838796205835692703)
XLA Ops:
  0.6 33.8 %dsgd.1 = (f32[640,256]{1,0:T(8,128)S(1)}, f32[128,256]{1,0:T(8,128)S(1)}) custom-call(s32[1,4]{1,0:T(1,128)} %cnt_hbm.1, f32[640,512]{1,0:T(8,128)} %r_hbm.1, s32[640,512]{1,0:T(8,128)} %m_hbm.1, f32[640,256]{1,0:T(8,128)} %u_hbm.1, f32[128,256]{1,0:T(8,128)} %v_hbm.1), custom_call_target="tpu_custom_call" | custom-call | tf_op jit(solution)/shard_map/dsgd/pallas_call | solution.py:216
  34.5 0.9 %flush.1 = (f32[640,256]{1,0:T(8,128)}, f32[128,256]{1,0:T(8,128)}) custom-call(f32[640,256]{1,0:T(8,128)S(1)} %get-tuple-element.4.u_vmem, f32[128,256]{1,0:T(8,128)S(1)} %get-tuple-element.5.v_vmem), custom_call_target="tpu_custom_call" | custom-call | tf_op jit(solution)/shard_map/flush/pallas_call | solution.py:240

commit v11 on v9

--- a/solution.py
+++ b/solution.py
@@ -9,6 +9,7 @@
 EPOCHS = 2
 STEPS_MAX = 4
 TILE = 256
+PIECE = 128
 
 
 def make_kernel(n, users, items, rank):
@@ -38,10 +39,12 @@
         for peer in (left, right):
             pl.semaphore_signal(barrier, inc=1, device_id={"shard": peer}, device_id_type=pl.DeviceIdType.MESH)
 
-        def block_copy(kind, q):
-            src, dst = ((r_hbm, r_buf), (m_hbm, m_buf))[kind]
+        def fetch_block(q):
             col = pl.multiple_of(lax.rem(me + q, n) * items, items)
-            return pltpu.make_async_copy(src.at[:, pl.ds(col, items)], dst.at[q], blk_sem.at[kind, min(q, 1)])
+            for s in range(0, users, PIECE):
+                for kind, (src, dst) in enumerate(((r_hbm, r_buf), (m_hbm, m_buf))):
+                    pltpu.make_async_copy(src.at[pl.ds(s, PIECE), pl.ds(col, items)], dst.at[q, pl.ds(s, PIECE)],
+                                          blk_sem.at[kind, min(q, 1)]).start()
 
         def block_wait(first, count):
             for kind, buf in enumerate((r_buf, m_buf)):
@@ -51,9 +54,9 @@
         u_in = pltpu.make_async_copy(u_hbm, u_out, u_sem)
         v_in = pltpu.make_async_copy(v_hbm, v_slot.at[0], v_sem)
         cnt_in = pltpu.make_async_copy(cnt_hbm, cnt, cnt_sem)
-        u_in.start()
-        block_copy(0, 0).start()
-        block_copy(1, 0).start()
+        for s in range(0, users, PIECE):
+            pltpu.make_async_copy(u_hbm.at[pl.ds(s, PIECE)], u_out.at[pl.ds(s, PIECE)], u_sem).start()
+        fetch_block(0)
         v_in.start()
         cnt_in.start()
 
@@ -71,8 +74,7 @@
             ut_b[:, pl.ds(s, 128)] = flipped.astype(bf16)
         block_wait(0, 1)
         for q in range(1, n):
-            block_copy(0, q).start()
-            block_copy(1, q).start()
+            fetch_block(q)
         flip_block(0)
         v_in.wait()
         cnt_in.wait()
@@ -191,11 +193,12 @@
 
 
 def flush(u_vmem, v_vmem, u_out, v_out, sem):
-    copies = [pltpu.make_async_copy(u_vmem, u_out, sem.at[0]), pltpu.make_async_copy(v_vmem, v_out, sem.at[1])]
-    for copy in copies:
-        copy.start()
-    for copy in copies:
-        copy.wait()
+    v_copy = pltpu.make_async_copy(v_vmem, v_out, sem.at[1])
+    v_copy.start()
+    for s in range(0, u_vmem.shape[0], PIECE):
+        pltpu.make_async_copy(u_vmem.at[pl.ds(s, PIECE)], u_out.at[pl.ds(s, PIECE)], sem.at[0]).start()
+    v_copy.wait()
+    pltpu.make_async_copy(u_vmem, u_out, sem.at[0]).wait()
 
 
 def solution(mesh):

time: 35.4 us -> 35.4 us (level)
  no operation moved by 1% of the time
where the time goes in v11:
time: 35.4 us; the launch traced here: 35.2 us
  Pallas kernels  34.6 us (98%)
  between operations  0.64 us (2%)
    pallas_call x1, Pallas kernels, local_run(): pl.pallas_call(make_kernel(n, users, items, rank), out_shape=(pltpu.VMEM(...  33.7 us
    pallas_call x1, Pallas kernels, local_run(): pl.pallas_call(flush, out_shape=(jax.ShapeDtypeStruct((users, rank), f32)...  0.89 us

profile of v11, /device:TPU:0, one launch (start us, length us, event | category | flops | bytes accessed | tf_op | source)
XLA Modules:
  0.0 35.2 jit_solution(10832171213717344089)
XLA Ops:
  0.6 33.7 %dsgd.1 = (f32[640,256]{1,0:T(8,128)S(1)}, f32[128,256]{1,0:T(8,128)S(1)}) custom-call(s32[1,4]{1,0:T(1,128)} %cnt_hbm.1, f32[640,512]{1,0:T(8,128)} %r_hbm.1, s32[640,512]{1,0:T(8,128)} %m_hbm.1, f32[640,256]{1,0:T(8,128)} %u_hbm.1, f32[128,256]{1,0:T(8,128)} %v_hbm.1), custom_call_target="tpu_custom_call" | custom-call | tf_op jit(solution)/shard_map/dsgd/pallas_call | solution.py:216
  34.3 0.9 %flush.1 = (f32[640,256]{1,0:T(8,128)}, f32[128,256]{1,0:T(8,128)}) custom-call(f32[640,256]{1,0:T(8,128)S(1)} %get-tuple-element.4.u_vmem, f32[128,256]{1,0:T(8,128)S(1)} %get-tuple-element.5.v_vmem), custom_call_target="tpu_custom_call" | custom-call | tf_op jit(solution)/shard_map/flush/pallas_call | solution.py:239

commit v12 on v9

--- a/solution.py
+++ b/solution.py
@@ -76,7 +76,6 @@
         flip_block(0)
         v_in.wait()
         cnt_in.wait()
-        pl.semaphore_wait(barrier, 2)
 
         def hop_copy(t, last=False):
             return pltpu.make_async_remote_copy(
@@ -84,13 +83,18 @@
                 send_sem=send_sem.at[lax.rem(t, 2)], recv_sem=recv_sem.at[lax.rem(t, n)],
                 device_id={"shard": left}, device_id_type=pl.DeviceIdType.MESH)
 
+        def when(condition, action):
+            if isinstance(condition, bool):
+                if condition:
+                    action()
+            else:
+                pl.when(condition)(action)
+
         def sub_epoch(t, carry):
             q = lax.rem(t, n)
             count = cnt[0, lax.rem(me + t, n)]
 
-            @pl.when(t > 0)
-            def _():
-                hop_copy(t - 1).wait_recv()
+            when(t > 0, lambda: hop_copy(t - 1).wait_recv())
 
             for k in range(STEPS_MAX):
                 v_old = (v_slot.at[t] if k == 0 else v_f)[...]
@@ -135,15 +139,11 @@
                     if k < STEPS_MAX - 1:
                         v_f[...] = v_new
                     else:
+                        if isinstance(t, int):
+                            pl.semaphore_wait(barrier, 2)
                         v_send[lax.rem(t, 2)] = v_new
-
-                        @pl.when(t < hops - 1)
-                        def _():
-                            hop_copy(t).start()
-
-                        @pl.when(t == hops - 1)
-                        def _():
-                            hop_copy(t, last=True).start()
+                        when(t < hops - 1, lambda: hop_copy(t).start())
+                        when(t == hops - 1, lambda: hop_copy(t, last=True).start())
 
                 def user_update(s, w):
                     cols = pl.ds(s, w)
@@ -167,21 +167,15 @@
                         for x in group:
                             piece(*x)
 
-            @pl.when(t == 0)
-            def _():
+            if isinstance(t, int):
                 block_wait(1, n - 1)
-
-            @pl.when(t + 1 < n)
-            def _():
-                flip_block(t + 1)
-
-            @pl.when(t > 0)
-            def _():
-                hop_copy(t - 1).wait_send()
+            when(t + 1 < n, lambda: flip_block(t + 1))
+            when(t > 0, lambda: hop_copy(t - 1).wait_send())
 
             return carry
 
-        lax.fori_loop(0, hops, sub_epoch, 0)
+        sub_epoch(0, 0)
+        lax.fori_loop(1, hops, sub_epoch, 0)
         for s in range(0, users, 128):
             u_out[pl.ds(s, 128), :] = ut_f[:, pl.ds(s, 128)].T
         hop_copy(hops - 1, last=True).wait_recv()

time: 35.4 us -> 35.3 us (level)
  no operation moved by 1% of the time
where the time goes in v12:
time: 35.3 us; the launch traced here: 35.2 us
  Pallas kernels  34.5 us (98%)
  between operations  0.64 us (2%)
    pallas_call x1, Pallas kernels, local_run(): pl.pallas_call(make_kernel(n, users, items, rank), out_shape=(pltpu.VMEM(...  33.6 us
    pallas_call x1, Pallas kernels, local_run(): pl.pallas_call(flush, out_shape=(jax.ShapeDtypeStruct((users, rank), f32)...  0.89 us

profile of v12, /device:TPU:0, one launch (start us, length us, event | category | flops | bytes accessed | tf_op | source)
XLA Modules:
  0.0 35.2 jit_solution(9343605190185744578)
XLA Ops:
  0.6 33.6 %dsgd.1 = (f32[640,256]{1,0:T(8,128)S(1)}, f32[128,256]{1,0:T(8,128)S(1)}) custom-call(s32[1,4]{1,0:T(1,128)} %cnt_hbm.1, f32[640,512]{1,0:T(8,128)} %r_hbm.1, s32[640,512]{1,0:T(8,128)} %m_hbm.1, f32[640,256]{1,0:T(8,128)} %u_hbm.1, f32[128,256]{1,0:T(8,128)} %v_hbm.1), custom_call_target="tpu_custom_call" | custom-call | tf_op jit(solution)/shard_map/dsgd/pallas_call | solution.py:207
  34.3 0.9 %flush.1 = (f32[640,256]{1,0:T(8,128)}, f32[128,256]{1,0:T(8,128)}) custom-call(f32[640,256]{1,0:T(8,128)S(1)} %get-tuple-element.4.u_vmem, f32[128,256]{1,0:T(8,128)S(1)} %get-tuple-element.5.v_vmem), custom_call_target="tpu_custom_call" | custom-call | tf_op jit(solution)/shard_map/flush/pallas_call | solution.py:230

commit v13 on v12

--- a/solution.py
+++ b/solution.py
@@ -64,18 +64,20 @@
                 r_t[q, :, cols] = marked
                 m_t[q, :, cols] = jnp.where(marked == marked, 1.0, 0.0).astype(bf16)
 
+        def flip_users():
+            for s in range(0, users, 128):
+                flipped = u_out[pl.ds(s, 128), :].T
+                ut_f[:, pl.ds(s, 128)] = flipped
+                ut_b[:, pl.ds(s, 128)] = flipped.astype(bf16)
+
         u_in.wait()
-        for s in range(0, users, 128):
-            flipped = u_out[pl.ds(s, 128), :].T
-            ut_f[:, pl.ds(s, 128)] = flipped
-            ut_b[:, pl.ds(s, 128)] = flipped.astype(bf16)
+        v_in.wait()
+        cnt_in.wait()
         block_wait(0, 1)
         for q in range(1, n):
             block_copy(0, q).start()
             block_copy(1, q).start()
         flip_block(0)
-        v_in.wait()
-        cnt_in.wait()
 
         def hop_copy(t, last=False):
             return pltpu.make_async_remote_copy(
@@ -114,25 +116,32 @@
                         return new
                     return jnp.where(jnp.full(new.shape, count, jnp.int32) > k, new, old)
 
+                fresh = isinstance(t, int) and k == 0
                 for s, w in tiles:
                     cols = pl.ds(s, w)
                     for a, h in split(w, items):
-                        approx = nn(v_half[a:a + h], ut_b[:, cols])
+                        if fresh:
+                            approx = nt(v_half[a:a + h], u_out[cols, :].astype(bf16))
+                        else:
+                            approx = nn(v_half[a:a + h], ut_b[:, cols])
                         err = (approx - r_t[q, pl.ds(a, h), cols]).astype(bf16)
                         seen = m_t[q, pl.ds(a, h), cols] > jnp.full((h, w), limit, f32).astype(bf16)
                         e_b[pl.ds(a, h), cols] = jnp.where(seen, err, jnp.zeros_like(err))
                 half = items // 2
                 parts = [keep * v_old[i * half:(i + 1) * half] for i in range(2)]
 
+                def times_users(err, cols):
+                    return nn(err, u_out[cols, :].astype(bf16)) if fresh else nt(err, ut_b[:, cols])
+
                 def item_grad(s, w):
                     cols = pl.ds(s, w)
                     if w == TILE:
-                        g = step_size * nt(e_b[:, cols], ut_b[:, cols])
+                        g = step_size * times_users(e_b[:, cols], cols)
                         for i in range(2):
                             parts[i] = parts[i] - g[i * half:(i + 1) * half]
                     else:
                         for i in range(2):
-                            parts[i] = parts[i] - step_size * nt(e_b[pl.ds(i * half, half), cols], ut_b[:, cols])
+                            parts[i] = parts[i] - step_size * times_users(e_b[pl.ds(i * half, half), cols], cols)
 
                 def item_update():
                     v_new = pick(jnp.concatenate(parts, axis=0), v_old)
@@ -154,6 +163,8 @@
                         ut_f[rows, cols] = u_new
                         ut_b[rows, cols] = u_new.astype(bf16)
 
+                if fresh:
+                    flip_users()
                 wide = [x for x in tiles if x[1] == TILE]
                 narrow = [x for x in tiles if x[1] < TILE]
                 if k < STEPS_MAX - 1:

time: 35.3 us -> 35 us (level)
  no operation moved by 1% of the time
where the time goes in v13:
time: 35 us; the launch traced here: 34.9 us
  Pallas kernels  34.3 us (98%)
  between operations  0.64 us (2%)
    pallas_call x1, Pallas kernels, local_run(): pl.pallas_call(make_kernel(n, users, items, rank), out_shape=(pltpu.VMEM(...  33.4 us
    pallas_call x1, Pallas kernels, local_run(): pl.pallas_call(flush, out_shape=(jax.ShapeDtypeStruct((users, rank), f32)...  0.89 us

profile of v13, /device:TPU:0, one launch (start us, length us, event | category | flops | bytes accessed | tf_op | source)
XLA Modules:
  0.0 34.9 jit_solution(12424042464513874097)
XLA Ops:
  0.6 33.4 %dsgd.1 = (f32[640,256]{1,0:T(8,128)S(1)}, f32[128,256]{1,0:T(8,128)S(1)}) custom-call(s32[1,4]{1,0:T(1,128)} %cnt_hbm.1, f32[640,512]{1,0:T(8,128)} %r_hbm.1, s32[640,512]{1,0:T(8,128)} %m_hbm.1, f32[640,256]{1,0:T(8,128)} %u_hbm.1, f32[128,256]{1,0:T(8,128)} %v_hbm.1), custom_call_target="tpu_custom_call" | custom-call | tf_op jit(solution)/shard_map/dsgd/pallas_call | solution.py:218
  34.0 0.9 %flush.1 = (f32[640,256]{1,0:T(8,128)}, f32[128,256]{1,0:T(8,128)}) custom-call(f32[640,256]{1,0:T(8,128)S(1)} %get-tuple-element.4.u_vmem, f32[128,256]{1,0:T(8,128)S(1)} %get-tuple-element.5.v_vmem), custom_call_target="tpu_custom_call" | custom-call | tf_op jit(solution)/shard_map/flush/pallas_call | solution.py:241
